TPU v7x, 128 devices: a whole 4x4x4 slice. The times are simulated.
128 devices in a mesh: mem: 8 (over z, y_lo), state: 16 (over y_hi, x, core).
Axes of the slice: x: 4, y: 4 (y_hi: 2, y_lo: 2; y = y_hi * 2 + y_lo), z: 4, core: 2. Of those that a mesh axis runs over, the one named last changes fastest.
Arguments:
- anomalies: bfloat16 [128, 32, 65536], P('mem', None, 'state'), may hold values from -0.75 to 0.75
- alpha: bfloat16 [128, 32, 2048], P('mem', None, 'state'), may hold values from -6 to 6
- basis: bfloat16 [2048, 65536], P(None, 'state'), may hold values from -0.1875 to 0.1875
- gradient: bfloat16 [32, 65536], P(None, 'state'), may hold values from -6 to 6
- vertical_root: float32 [32, 32], replicated, may hold values from -1 to 1
- band_gain: float32 [16], replicated, may hold values from 0.25 to 2
- band: int32 [2048], P('state'), may hold values from 0 to 15
- order: int32 [128], replicated, may hold values from 0 to 127, each once
Outputs:
- increment: float32 [32, 65536], P(None, 'state')
- alpha_grad: float32 [128, 32, 2048], P('mem', None, 'state')
Inputs may be any that keep to these rules, and one draw needn't show every extreme that they name: `order`: a permutation: every member is named by exactly one slot.
All inputs are finite; a program needn't handle non-finite values.
Results may differ from a plain program's by a relative error of at most 0.0029.
Values may be sent and summed in bfloat16 or wider, within the bound.
A program may use at most 128 MiB of HBM per device.

v0:
```python
import jax
import jax.numpy as jnp
from jax import lax
from jax.sharding import PartitionSpec as P


def from_everyone(array, axis):
    count = lax.axis_size(axis)
    return lax.all_to_all(
        jnp.broadcast_to(array[None], (count, *array.shape)), axis, 0, 0, tiled=True
    )


def in_order(pieces, dim):
    lengths = list(pieces.shape[1:])
    lengths[dim] *= pieces.shape[0]
    return jnp.moveaxis(pieces, 0, dim).reshape(lengths)


def gathered_copies(array, axis, dim):
    pieces = from_everyone(array, axis)
    return in_order(pieces, dim)


def taken_together(array, axis):
    return from_everyone(array, axis).sum(axis=0)


def on_device(anomalies, alpha, basis, gradient, vertical_root, band_gain, band, order):
    high = lax.Precision.HIGHEST
    mem_count = lax.axis_size("mem")
    mem_rank = lax.axis_index("mem")
    member_dev, levels, columns = anomalies.shape
    mode_rows = alpha.shape[2]
    bands = band_gain.shape[0]
    onehot = (band[:, None] == jnp.arange(bands, dtype=jnp.int32)[None, :]).astype(jnp.float32)
    filter_gain = jnp.sum(onehot * band_gain[None, :], axis=1)
    coef = jnp.einsum("ab,jbk->jak", vertical_root, alpha.astype(jnp.float32), precision=high)
    coef = (coef * filter_gain[None, None, :]).astype(jnp.bfloat16)
    members = mem_rank * member_dev + jnp.arange(member_dev, dtype=jnp.int32)
    select = (order[None, :] == members[:, None]).astype(jnp.bfloat16)
    slot_coef = gathered_copies(coef, "mem", 0)
    own_coef = jnp.einsum("ij,jlc->ilc", select, slot_coef, preferred_element_type=jnp.float32)
    own_coef = own_coef.astype(jnp.bfloat16).reshape(member_dev * levels, mode_rows)
    basis_rows = basis
    member_field = jnp.dot(
        gathered_copies(own_coef, "state", 1), basis_rows, preferred_element_type=jnp.float32
    )
    partial_value = jnp.sum(
        anomalies.astype(jnp.float32) * member_field.reshape(member_dev, levels, columns), axis=0
    )
    increment = taken_together(partial_value, "mem")
    weighted = (anomalies.astype(jnp.float32) * gradient.astype(jnp.float32)[None]).astype(
        jnp.bfloat16
    )
    weighted = weighted.reshape(member_dev * levels, columns)
    basis_rows = basis
    projected = lax.psum_scatter(
        lax.dot_general(
            basis_rows, weighted, (((1,), (1,)), ((), ())), preferred_element_type=jnp.float32
        ),
        "state",
        scatter_dimension=0,
        tiled=True,
    )
    member_grad = jnp.einsum(
        "ab,kma->mbk",
        vertical_root,
        projected.reshape(mode_rows, member_dev, levels),
        precision=high,
    )
    member_grad = member_grad * filter_gain[None, None, :]
    placed = jnp.einsum("ij,ibk->jbk", select.astype(jnp.float32), member_grad, precision=high)
    outgoing = placed.reshape(mem_count, member_dev, levels, mode_rows)
    incoming = lax.all_to_all(outgoing, "mem", split_axis=0, concat_axis=0, tiled=True)
    alpha_grad = jnp.sum(incoming, axis=0)
    return (increment, alpha_grad)


def solution(mesh):
    return jax.shard_map(
        on_device,
        mesh=mesh,
        in_specs=(
            P("mem", None, "state"),
            P("mem", None, "state"),
            P(None, "state"),
            P(None, "state"),
            P(),
            P(),
            P("state"),
            P(),
        ),
        out_specs=(P(None, "state"), P("mem", None, "state")),
        check_vma=False,
    )
```

profile of v0, /device:TPU:0, one launch (start us, length us, event | category | flops | bytes accessed | tf_op | source)
XLA Modules:
  0.0 192.5 jit_solution(12334071255457948951)
XLA Ops:
  7.2 0.0 copy-start
  7.2 0.8 select_reduce_fusion
  8.0 0.1 copy-done
  8.1 1.0 fusion.8
  9.1 0.1 copy.22
  9.1 1.1 broadcast_in_dim.8
  10.3 6.4 %all-to-all-start = ((bf16[8,16,32,128]{3,1,2,0:T(8,128)(2,1)}), bf16[8,16,32,128]{3,1,2,0:T(8,128)(2,1)S(1)}, u32[]{:S(2)}, u32[]{:S(2)}) async-start(bf16[8,16,32,128]{3,1,2,0:T(8,128)(2,1)} %broadcast_in_dim.8), calls=%async_computation | async-start | bytes 2097152 | tf_op jit(solution)/shard_map/all_to_all | solution.py:9
  16.7 1.0 convert_element_type.27
  17.7 0.0 copy-start.2
  17.7 5.3 %fusion.3 = bf16[16,32,4096]{2,1,0:T(8,128)(2,1)} fusion(bf16[16,32,4096]{2,1,0:T(8,128)(2,1)} %param.8, f32[32,4096]{1,0:T(8,128)S(1)} %convert_element_type.27), kind=kLoop, calls=%fused_computation.5 | loop fusion | flops 6291456 | bytes 8912896 | tf_op jit(solution)/shard_map/convert_element_type | solution.py:53
  23.0 9.4 %all-to-all-done = bf16[8,16,32,128]{3,1,2,0:T(8,128)(2,1)S(1)} async-done(((bf16[8,16,32,128]{3,1,2,0:T(8,128)(2,1)}), bf16[8,16,32,128]{3,1,2,0:T(8,128)(2,1)S(1)}, u32[]{:S(2)}, u32[]{:S(2)}) %all-to-all-start) | async-done | bytes 1048608 | tf_op jit(solution)/shard_map/all_to_all | solution.py:9
  32.4 0.3 copy.23
  32.7 0.0 copy-done.2
  32.7 0.3 convolution_convert_fusion
  33.1 1.8 broadcast_in_dim.10
  34.9 6.8 %all-to-all-start.1 = ((bf16[16,512,128]{2,1,0:T(8,128)(2,1)}), bf16[16,512,128]{2,1,0:T(8,128)(2,1)S(1)}, u32[]{:S(2)}, u32[]{:S(2)}) async-start(bf16[16,512,128]{2,1,0:T(8,128)(2,1)} %broadcast_in_dim.10), calls=%async_computation.1 | async-start | bytes 4194304 | tf_op jit(solution)/shard_map/all_to_all | solution.py:9
  41.6 0.0 reduce-scatter.2.cloned.1.call-start
  41.7 15.0 %convolution_bitcast_fusion = f32[2048,512]{0,1:T(8,128)} fusion(bf16[512,4096]{1,0:T(8,128)(2,1)} %bitcast.36, bf16[2048,4096]{1,0:T(8,128)(2,1)} %param.10), kind=kOutput, calls=%fused_computation.6 | convolution fusion | flops 8589934592 | bytes 25165824 | tf_op jit(solution)/shard_map/dot_general | solution.py:59
  56.7 0.0 reduce-scatter.2.cloned.1.call-update
  56.7 14.1 %all-to-all-done.1 = bf16[16,512,128]{2,1,0:T(8,128)(2,1)S(1)} async-done(((bf16[16,512,128]{2,1,0:T(8,128)(2,1)}), bf16[16,512,128]{2,1,0:T(8,128)(2,1)S(1)}, u32[]{:S(2)}, u32[]{:S(2)}) %all-to-all-start.1) | async-done | bytes 2097184 | tf_op jit(solution)/shard_map/all_to_all | solution.py:9
  70.8 2.7 %copy.25 = bf16[512,16,128]{2,1,0:T(8,128)(2,1)} copy(bf16[512,16,128]{2,0,1:T(8,128)(2,1)S(1)} %bitcast.34) | data formatting | bytes 4194304 | tf_op jit(solution)/shard_map/transpose | solution.py:17
  73.5 2.9 %dot_general.24 = bf16[16,32,2048]{2,1,0:T(8,128)(2,1)S(1)} reshape(bf16[512,16,128]{2,1,0:T(8,128)(2,1)} %copy.25) | data formatting | bytes 4194304 | tf_op jit(solution)/shard_map/dot_general | solution.py:46
  76.4 13.4 %fusion.2 = f32[32,4096]{1,0:T(8,128)S(1)} fusion(bf16[16,32,4096]{2,1,0:T(8,128)(2,1)} %param.8, bf16[16,32,2048]{2,1,0:T(8,128)(2,1)S(1)} %dot_general.24, bf16[2048,4096]{1,0:T(8,128)(2,1)} %param.10), kind=kOutput, calls=%fused_computation.4 | convolution fusion | flops 8596094976 | bytes 23592960 | tf_op jit(solution)/shard_map/dot_general | solution.py:46
  89.8 2.5 %broadcast_in_dim.11 = f32[8,32,4096]{2,1,0:T(8,128)} broadcast(f32[32,4096]{1,0:T(8,128)S(1)} %fusion.2), dimensions={1,2} | broadcast | bytes 4718592 | tf_op jit(solution)/shard_map/broadcast_in_dim | solution.py:10
  92.2 0.0 copy-start.1
  92.2 4.7 %all-to-all-start.2 = ((f32[8,32,4096]{2,1,0:T(8,128)}), f32[8,32,4096]{2,1,0:T(8,128)}, u32[]{:S(2)}, u32[]{:S(2)}) async-start(f32[8,32,4096]{2,1,0:T(8,128)} %broadcast_in_dim.11), calls=%async_computation.2 | async-start | bytes 8388608 | tf_op jit(solution)/shard_map/all_to_all | solution.py:9
  96.9 49.9 %reduce-scatter.2.cloned.1.call-done = f32[128,512]{0,1:T(8,128)} async-done(((f32[2048,512]{0,1:T(8,128)}), f32[128,512]{0,1:T(8,128)}) %reduce-scatter.2.cloned.1.call-update) | async-done | bytes 262160 | tf_op jit(solution)/shard_map/reduce_scatter | solution.py:58
  146.8 0.0 copy-done.1
  146.8 1.4 fusion.6
  148.2 1.1 fusion.9
  149.3 1.5 copy.28
  150.8 3.1 %all-to-all-done.2 = f32[8,32,4096]{2,1,0:T(8,128)} async-done(((f32[8,32,4096]{2,1,0:T(8,128)}), f32[8,32,4096]{2,1,0:T(8,128)}, u32[]{:S(2)}, u32[]{:S(2)}) %all-to-all-start.2) | async-done | bytes 4194336 | tf_op jit(solution)/shard_map/all_to_all | solution.py:9
  153.9 3.6 %all-to-all-start.3 = ((f32[8,16,32,128]{3,1,2,0:T(8,128)}), f32[8,16,32,128]{3,1,2,0:T(8,128)S(1)}, u32[]{:S(2)}, u32[]{:S(2)}) async-start(f32[8,16,32,128]{3,1,2,0:T(8,128)} %copy.28), calls=%async_computation.4 | async-start | bytes 4194304 | tf_op jit(solution)/shard_map/all_to_all | solution.py:75
  157.5 3.2 %reduce_sum.38 = f32[32,4096]{1,0:T(8,128)} reduce(f32[8,32,4096]{2,1,0:T(8,128)} %all-to-all-done.2, f32[]{:T(128)} %constant.10.clone.1), dimensions={0}, to_apply=%region_2.0 | reduce | flops 917504 | bytes 4718596 | tf_op jit(solution)/shard_map/reduce_sum | solution.py:26
  160.8 23.9 %all-to-all-done.3 = f32[8,16,32,128]{3,1,2,0:T(8,128)S(1)} async-done(((f32[8,16,32,128]{3,1,2,0:T(8,128)}), f32[8,16,32,128]{3,1,2,0:T(8,128)S(1)}, u32[]{:S(2)}, u32[]{:S(2)}) %all-to-all-start.3) | async-done | bytes 2097184 | tf_op jit(solution)/shard_map/all_to_all | solution.py:75
  184.7 0.1 reduce_sum.39
  184.8 0.8 copy.30
  (2 shorter events, 0.0 us)
Async XLA Ops:
  7.2 0.9 copy-start
  10.3 22.1 %all-to-all-start = ((bf16[8,16,32,128]{3,1,2,0:T(8,128)(2,1)}), bf16[8,16,32,128]{3,1,2,0:T(8,128)(2,1)S(1)}, u32[]{:S(2)}, u32[]{:S(2)}) async-start(bf16[8,16,32,128]{3,1,2,0:T(8,128)(2,1)} %broadcast_in_dim.8), calls=%async_computation | async-start | bytes 2097152 | tf_op jit(solution)/shard_map/all_to_all | solution.py:9
  17.7 15.0 %copy-start.2 = (s32[128]{0:T(128)S(1)}, s32[128]{0:T(128)}, u32[]{:S(2)}) copy-start(s32[128]{0:T(128)} %param.15) | copy-start | bytes 1540
  34.9 36.0 %all-to-all-start.1 = ((bf16[16,512,128]{2,1,0:T(8,128)(2,1)}), bf16[16,512,128]{2,1,0:T(8,128)(2,1)S(1)}, u32[]{:S(2)}, u32[]{:S(2)}) async-start(bf16[16,512,128]{2,1,0:T(8,128)(2,1)} %broadcast_in_dim.10), calls=%async_computation.1 | async-start | bytes 4194304 | tf_op jit(solution)/shard_map/all_to_all | solution.py:9
  41.6 105.2 %reduce-scatter.2.cloned.1.call-start = ((), (), s32[]{:S(2)}) async-start(), calls=%async_computation.5 | async-start | bytes 4456448 | tf_op jit(solution)/shard_map/reduce_scatter | solution.py:58
  92.2 54.6 %copy-start.1 = (f32[32,32]{1,0:T(8,128)S(1)}, f32[32,32]{1,0:T(8,128)}, u32[]{:S(2)}) copy-start(f32[32,32]{1,0:T(8,128)} %param.12) | copy-start | bytes 12292
  92.2 61.7 %all-to-all-start.2 = ((f32[8,32,4096]{2,1,0:T(8,128)}), f32[8,32,4096]{2,1,0:T(8,128)}, u32[]{:S(2)}, u32[]{:S(2)}) async-start(f32[8,32,4096]{2,1,0:T(8,128)} %broadcast_in_dim.11), calls=%async_computation.2 | async-start | bytes 8388608 | tf_op jit(solution)/shard_map/all_to_all | solution.py:9
  153.9 30.8 %all-to-all-start.3 = ((f32[8,16,32,128]{3,1,2,0:T(8,128)}), f32[8,16,32,128]{3,1,2,0:T(8,128)S(1)}, u32[]{:S(2)}, u32[]{:S(2)}) async-start(f32[8,16,32,128]{3,1,2,0:T(8,128)} %copy.28), calls=%async_computation.4 | async-start | bytes 4194304 | tf_op jit(solution)/shard_map/all_to_all | solution.py:75
Sparse Core Ops, SparseCore 0:
  56.8 89.9 reduce-scatter.1
where the time goes:
time: 193 us; the launch traced here: 192 us
  waiting for transfers between devices  100 us (52%)
  matrix products  32.1 us (17%)
  starting transfers between devices  21.5 us (11%)
  between operations  14.2 us (7%)
  local copies, waits for them, and re-layouts  13.8 us (7%)
  other arithmetic  10.5 us (5%)
    reduce_scatter x1, waiting for transfers between devices, on_device(): lax.psum_scatter(lax.dot_general(basis_rows, weighted, (((1,), (1,)), (()...  49.9 us
    all_to_all x3, waiting for transfers between devices, from_everyone(): lax.all_to_all(jnp.broadcast_to(array[None], (count, *array.shape)), axis...  26.6 us
    all_to_all x1, waiting for transfers between devices, on_device(): lax.all_to_all(outgoing, 'mem', split_axis=0, concat_axis=0, tiled=True)  23.9 us
    all_to_all x3, starting transfers between devices, from_everyone(): lax.all_to_all(jnp.broadcast_to(array[None], (count, *array.shape)), axis...  17.9 us
    dot_general x1, matrix products, on_device(): lax.dot_general(basis_rows, weighted, (((1,), (1,)), ((), ())), preferred...  15 us
    dot_general x1, matrix products, on_device(): jnp.dot(gathered_copies(own_coef, 'state', 1), basis_rows, preferred_elem...  13.4 us
    broadcast_in_dim x3, local copies, waits for them, and re-layouts, from_everyone(): jnp.broadcast_to(array[None], (count, *array.shape))  5.38 us
    convert_element_type x1, other arithmetic, on_device(): (anomalies.astype(jnp.float32) * gradient.astype(jnp.float32)[None]).asty...  5.32 us
  transfers between devices with their start and end apart: 5, of which 5 were waited for; matrix products, arithmetic and copies ran while one was open for 26% of the time, Pallas kernels for 0%

commit v1 on v0

v1 whole, which is shorter than its diff:
```python
import functools

import jax
import jax.numpy as jnp
from jax import lax
from jax.experimental import pallas as pl
from jax.experimental.pallas import tpu as pltpu
from jax.sharding import PartitionSpec as P

MESH = pl.DeviceIdType.MESH
NT = (((1,), (1,)), ((), ()))
HIGH = lax.Precision.HIGHEST
F32 = jnp.float32
BF16 = jnp.bfloat16


def kernel(
    order, inverse, gains, anom_hbm, alpha, basis_hbm, grad, root, band,
    inc_out, ag_out,
    basis, anom, weighted, part, half, outgo, landed, coefs, zall, ypart, ysend,
    inc_acc, inc_send, inc_land, inc_own, gall, gpart, gsend,
    load_sem, asem, z_s, z_r, y_s, y_r, b_s, b_r, d_s, d_r, x_s, x_r, r_s, r_r,
    i_s, i_r, o_s, o_r, gz_s, gz_r, gy_s, gy_r,
):
    m = lax.axis_index("mem")
    s = lax.axis_index("state")
    z, yl = m // 2, m % 2
    chip, core = s // 2, s % 2
    yh, x = chip // 4, chip % 4
    other = 1 - core

    def chip_at(t):
        return ((yh + t // 4) % 2) * 4 + (x + t % 4) % 4

    def mem_at(u):
        return ((z + u // 2) % 4) * 2 + (yl + u % 2) % 2

    def back(t):
        return (t // 4) * 4 + (4 - t % 4) % 4

    def remote(src, dst, send, recv, mem, state):
        return pltpu.make_async_remote_copy(
            src_ref=src, dst_ref=dst, send_sem=send, recv_sem=recv,
            device_id=(mem, state), device_id_type=MESH,
        )

    def lanes(start, width):
        return pl.ds(pl.multiple_of(start, 128), width)

    partner = chip * 2 + other
    ymate = z * 2 + (1 - yl)

    def load(r):
        q = chip_at(7 - r)
        return pltpu.make_async_copy(
            basis_hbm.at[pl.ds(pl.multiple_of(q * 256, 256), 256), :],
            basis.at[pl.ds(pl.multiple_of(r * 256, 256), 256), :],
            load_sem.at[r],
        )

    def load_anom(g):
        rows = pl.ds(g * 128, 128)
        return pltpu.make_async_copy(anom_hbm.at[rows, :], anom.at[rows, :], asem.at[g])

    for g in range(4):
        load_anom(g).start()
    load(0).start()
    load(1).start()

    barrier = pltpu.get_barrier_semaphore()
    for u in range(1, 8):
        pl.semaphore_signal(barrier, inc=1, device_id=(mem_at(u), s), device_id_type=MESH)
        pl.semaphore_signal(
            barrier, inc=1, device_id=(m, chip_at(u) * 2 + core), device_id_type=MESH
        )
    pl.semaphore_signal(barrier, inc=1, device_id=(m, partner), device_id_type=MESH)

    bands = band[...]
    gain = jnp.zeros((1, 128), F32)
    for b in range(16):
        gain = jnp.where(bands == b, gains[b], gain)
    rooted = jnp.concatenate([root[...]] * 4, axis=0)
    rooted = jnp.concatenate([rooted] * 4, axis=1)
    row = lax.broadcasted_iota(jnp.int32, (128, 128), 0) // 32
    col = lax.broadcasted_iota(jnp.int32, (128, 128), 1) // 32
    rooted = jnp.where(row == col, rooted, 0.0)
    for g in range(4):
        block = alpha[g * 4:(g + 1) * 4].astype(F32).reshape(128, 128)
        value = jnp.dot(rooted, block, precision=HIGH, preferred_element_type=F32) * gain
        zall[pl.ds(z * 16 + g * 4, 4)] = value.astype(BF16).reshape(4, 32, 128)

    pl.semaphore_wait(barrier, 15)

    def z_copy(all_ref, dz, send, recv, got):
        mine = all_ref.at[pl.ds(z * 16, 16)]
        dst = all_ref.at[pl.ds(((z + 4 - dz) % 4) * 16, 16)] if got else mine
        return remote(mine, dst, send.at[dz - 1], recv.at[dz - 1], ((z + dz) % 4) * 2 + yl, s)

    for dz in (1, 3, 2):
        z_copy(zall, dz, z_s, z_r, False).start()

    for g in range(4):
        load_anom(g).wait()

        def weigh(c, carry):
            w = lanes(c * 512, 512)
            factor = grad[:, w].astype(F32)
            for k in range(4):
                rows = pl.ds(g * 128 + k * 32, 32)
                weighted[rows, w] = (anom[rows, w].astype(F32) * factor).astype(BF16)
            return carry

        lax.fori_loop(0, 8, weigh, 0)

    def pick(table, all_ref, slot):
        where = table[slot]
        same = (where // 16) % 2 == yl
        return same, all_ref[(where // 32) * 16 + where % 16]

    def y_copy(src, dst, send, recv):
        return remote(src, dst, send.at[0], recv.at[0], ymate, s)

    def b_block(r):
        return coefs.at[:, lanes(r * 256 + core * 128, 128)]

    def b_copy(t):
        return remote(
            b_block(7), b_block(7 - back(t)), b_s.at[7 - t], b_r.at[7 - back(t)],
            m, chip_at(t) * 2 + core,
        )

    def d_copy(r):
        return remote(b_block(r), b_block(r), d_s.at[r], d_r.at[r], m, partner)

    def d_got(r):
        there = coefs.at[:, lanes(r * 256 + other * 128, 128)]
        return remote(there, there, d_s.at[r], d_r.at[r], m, partner)

    def x_copy(r):
        return remote(
            part.at[r, :, lanes(other * 128, 128)], half.at[r], x_s.at[r], x_r.at[r], m, partner
        )

    def r_copy(r):
        return remote(
            outgo.at[r], landed.at[r], r_s.at[r], r_r.at[r], m, chip_at(7 - r) * 2 + core
        )

    def adjoint(r, carry):
        @pl.when(r < 6)
        def _():
            load(r + 2).start()

        load(r).wait()
        rows = pl.ds(pl.multiple_of(r * 256, 256), 256)
        part[r] = lax.dot_general(weighted[...], basis[rows, :], NT, preferred_element_type=F32)
        x_copy(r).start()

        @pl.when(r > 0)
        def _():
            p = r - 1
            x_copy(p).wait_recv()
            outgo[p] = (part[p, :, lanes(core * 128, 128)] + half[p]).astype(BF16)
            r_copy(p).start()

        @pl.when(r == 3)
        def _():
            for dz in (1, 3, 2):
                z_copy(zall, dz, z_s, z_r, True).wait_recv()
            for i in range(16):
                same, value = pick(inverse, zall, ymate * 16 + i)
                ysend[i] = jnp.where(same, value, jnp.zeros_like(value))
            y_copy(ysend, ypart, y_s, y_r).start()

        @pl.when(r == 5)
        def _():
            y_copy(ysend, ypart, y_s, y_r).wait_recv()
            for i in range(16):
                same, value = pick(inverse, zall, m * 16 + i)
                coefs[pl.ds(i * 32, 32), lanes(7 * 256 + core * 128, 128)] = jnp.where(
                    same, value, ypart[i]
                )
            d_copy(7).start()
            for t in (1, 3, 2, 4, 5, 7, 6):
                b_copy(t).start()

        return carry

    lax.fori_loop(0, 8, adjoint, 0)

    def b_got(r):
        return remote(b_block(r), b_block(r), b_s.at[r], b_r.at[r], m, s)

    def pass_on(r):
        remote(
            b_block(7), b_block(r), b_s.at[r], b_r.at[r], m, chip_at(7 - r) * 2 + core
        ).wait_recv()
        d_copy(r).start()

    def field_part(low, c):
        w = lanes(c * 512, 512)
        f = jnp.dot(coefs[:, low:low + 1024], basis[low:low + 1024, w], preferred_element_type=F32)
        return w, jnp.sum((f * anom[:, w].astype(F32)).reshape(16, 32, 512), axis=0)

    for r in (4, 5, 6):
        pass_on(r)
    for r in (7, 4, 5, 6):
        d_got(r).wait_recv()

    def near(c, carry):
        w, value = field_part(1024, c)
        inc_acc[:, w] = value

        @pl.when(c == 4)
        def _():
            for r in range(4):
                pass_on(r)

        return carry

    lax.fori_loop(0, 8, near, 0)

    x_copy(7).wait_recv()
    for r in range(7):
        r_copy(r).wait_recv()
    for g in range(4):
        rows = pl.ds(g * 128, 128)
        total = part[7, rows, lanes(core * 128, 128)] + half[7, rows, :]
        for r in range(7):
            total = total + landed[r, rows, :].astype(F32)
        value = jnp.dot(rooted.T, total, precision=HIGH, preferred_element_type=F32) * gain
        gall[pl.ds(z * 16 + g * 4, 4)] = value.astype(BF16).reshape(4, 32, 128)
    for dz in (1, 3, 2):
        z_copy(gall, dz, gz_s, gz_r, False).start()

    for r in range(4):
        d_got(r).wait_recv()

    def i_copy(i):
        return remote(inc_send.at[i], inc_land.at[i], i_s.at[i], i_r.at[i], mem_at(7 - i), s)

    def far(i, carry):
        w, value = field_part(0, mem_at(7 - i))
        inc_send[i] = value + inc_acc[:, w]

        @pl.when(i < 7)
        def _():
            i_copy(i).start()

        @pl.when(i == 5)
        def _():
            for dz in (1, 3, 2):
                z_copy(gall, dz, gz_s, gz_r, True).wait_recv()
            for k in range(16):
                same, got = pick(order, gall, ymate * 16 + k)
                gsend[k] = jnp.where(same, got, jnp.zeros_like(got))
            y_copy(gsend, gpart, gy_s, gy_r).start()

        return carry

    lax.fori_loop(0, 8, far, 0)

    total = inc_send[7]
    for i in range(7):
        i_copy(i).wait_recv()
        total = total + inc_land[i]
    inc_own[...] = total

    def o_copy(u, got):
        target = mem_at(u)
        spot = mem_at(((4 - u // 2) % 4) * 2 + u % 2) if got else m
        return remote(
            inc_own, inc_out.at[:, lanes(spot * 512, 512)], o_s.at[u - 1], o_r.at[u - 1], target, s
        )

    for u in (4, 5, 1, 2, 3, 6, 7):
        o_copy(u, False).start()
    inc_out[:, lanes(m * 512, 512)] = total

    y_copy(gsend, gpart, gy_s, gy_r).wait_recv()
    for i in range(16):
        same, value = pick(order, gall, m * 16 + i)
        ag_out[i] = jnp.where(same, value, gpart[i]).astype(F32)

    for u in range(1, 8):
        o_copy(u, True).wait_recv()

    for dz in (1, 2, 3):
        z_copy(zall, dz, z_s, z_r, False).wait_send()
        z_copy(gall, dz, gz_s, gz_r, False).wait_send()
    y_copy(ysend, ypart, y_s, y_r).wait_send()
    y_copy(gsend, gpart, gy_s, gy_r).wait_send()
    for t in range(1, 8):
        b_copy(t).wait_send()
        r_copy(t - 1).wait_send()
        i_copy(t - 1).wait_send()
        o_copy(t, False).wait_send()
    for r in range(8):
        d_copy(r).wait_send()
        x_copy(r).wait_send()


def on_device(anomalies, alpha, basis, gradient, vertical_root, band_gain, band, order):
    members, levels, columns = anomalies.shape
    slots = jnp.arange(order.shape[0], dtype=jnp.int32)
    inverse = jnp.sum(jnp.where(order[None, :] == slots[:, None], slots[None, :], 0), axis=1)
    vmem, smem = pl.BlockSpec(memory_space=pltpu.VMEM), pl.BlockSpec(memory_space=pltpu.SMEM)
    hbm = pl.BlockSpec(memory_space=pl.ANY)
    dma = lambda n: pltpu.SemaphoreType.DMA((n,))
    return pl.pallas_call(
        kernel,
        out_shape=(
            jax.ShapeDtypeStruct((32, 4096), F32),
            jax.ShapeDtypeStruct((16, 32, 128), F32),
        ),
        in_specs=[smem, smem, smem, hbm, vmem, hbm, vmem, vmem, vmem],
        out_specs=(vmem, vmem),
        scratch_shapes=[
            pltpu.VMEM((2048, 4096), BF16),
            pltpu.VMEM((512, 4096), BF16),
            pltpu.VMEM((512, 4096), BF16),
            pltpu.VMEM((8, 512, 256), F32),
            pltpu.VMEM((8, 512, 128), F32),
            pltpu.VMEM((7, 512, 128), BF16),
            pltpu.VMEM((7, 512, 128), BF16),
            pltpu.VMEM((512, 2048), BF16),
            pltpu.VMEM((64, 32, 128), BF16),
            pltpu.VMEM((16, 32, 128), BF16),
            pltpu.VMEM((16, 32, 128), BF16),
            pltpu.VMEM((32, 4096), F32),
            pltpu.VMEM((8, 32, 512), F32),
            pltpu.VMEM((7, 32, 512), F32),
            pltpu.VMEM((32, 512), F32),
            pltpu.VMEM((64, 32, 128), BF16),
            pltpu.VMEM((16, 32, 128), BF16),
            pltpu.VMEM((16, 32, 128), BF16),
            dma(8), dma(4), dma(3), dma(3), dma(1), dma(1), dma(7), dma(7), dma(8), dma(8),
            dma(8), dma(8), dma(7), dma(7), dma(7), dma(7), dma(7), dma(7), dma(3), dma(3),
            dma(1), dma(1),
        ],
        compiler_params=pltpu.CompilerParams(
            collective_id=0, has_side_effects=True, vmem_limit_bytes=60 << 20
        ),
    )(
        order, inverse, band_gain, anomalies.reshape(members * levels, columns), alpha, basis,
        gradient, vertical_root, band.reshape(1, -1),
    )


def solution(mesh):
    return jax.shard_map(
        on_device,
        mesh=mesh,
        in_specs=(
            P("mem", None, "state"),
            P("mem", None, "state"),
            P(None, "state"),
            P(None, "state"),
            P(),
            P(),
            P("state"),
            P(),
        ),
        out_specs=(P(None, "state"), P("mem", None, "state")),
        check_vma=False,
    )
```

time: 193 us -> 78.9 us (0.41)
  waiting for transfers between devices: 100 us -> 0 us
  Pallas kernels: 0 us -> 73.2 us
  matrix products: 32.1 us -> 0 us
  starting transfers between devices: 21.5 us -> 0 us
  between operations: 14.2 us -> 0.64 us
  local copies, waits for them, and re-layouts: 13.8 us -> 3.54 us
  other arithmetic: 10.5 us -> 1.28 us
    pallas_call x0 -> x1, Pallas kernels: none -> 73.2 us  [on_device(): pl.pallas_call(kernel, out_shape=(jax.ShapeDtypeStruct((32, 4096), F32),...]
    all_to_all x4 -> x0, waiting for transfers between devices: 50.5 us -> none  [the longest x3 26.6 us: from_everyone(): lax.all_to_all(jnp.broadcast_to(array[None], (count, *array.shape)), axis...]
    reduce_scatter x1 -> x0, waiting for transfers between devices: 49.9 us -> none  [on_device(): lax.psum_scatter(lax.dot_general(basis_rows, weighted, (((1,), (1,)), (()...]
    dot_general x6 -> x0, matrix products: 32.1 us -> none  [the longest x1 15 us: on_device(): lax.dot_general(basis_rows, weighted, (((1,), (1,)), ((), ())), preferred...]
    all_to_all x4 -> x0, starting transfers between devices: 21.5 us -> none  [the longest x3 17.9 us: from_everyone(): lax.all_to_all(jnp.broadcast_to(array[None], (count, *array.shape)), axis...]
    convert_element_type x2 -> x0, other arithmetic: 6.3 us -> none  [the longest x1 5.32 us: on_device(): (anomalies.astype(jnp.float32) * gradient.astype(jnp.float32)[None]).asty...]
    broadcast_in_dim x3 -> x0, local copies, waits for them, and re-layouts: 5.38 us -> none  [from_everyone(): jnp.broadcast_to(array[None], (count, *array.shape))]
    reduce_sum x3 -> x1, other arithmetic: 4.18 us -> 1.28 us  [on_device(): jnp.sum(jnp.where(order[None, :] == slots[:, None], slots[None, :], 0), a...]
  transfers between devices with their start and end apart: 5 -> 0, of which waited for: 5 -> 0; matrix products, arithmetic and copies ran while one was open for 26% -> 0% of each run, Pallas kernels for 0% -> 0%
where the time goes in v1:
time: 78.9 us; the launch traced here: 78.7 us
  Pallas kernels  73.2 us (93%)
  local copies, waits for them, and re-layouts  3.54 us (4%)
  other arithmetic  1.28 us (2%)
    pallas_call x1, Pallas kernels, on_device(): pl.pallas_call(kernel, out_shape=(jax.ShapeDtypeStruct((32, 4096), F32),...  73.2 us
    unnamed x2, local copies, waits for them, and re-layouts  3.54 us

profile of v1, /device:TPU:0, one launch (start us, length us, event | category | flops | bytes accessed | tf_op | source)
XLA Modules:
  0.0 78.7 jit_solution(10576814436448749065)
XLA Ops:
  0.6 1.3 %select_reduce_fusion.inverse = s32[128]{0:T(128)} fusion(s32[128]{0:T(128)} %order.1), kind=kLoop, calls=%fused_computation | loop fusion | flops 49024 | bytes 1024 | tf_op jit(solution)/shard_map/reduce_sum | solution.py:306
  1.9 73.2 %shard_map.95 = (f32[32,4096]{1,0:T(8,128)}, f32[16,32,128]{2,1,0:T(8,128)}) custom-call(s32[128]{0:T(128)} %order.1, s32[128]{0:T(128)} %select_reduce_fusion.inverse, f32[16]{0:T(128)} %gains.1, bf16[512,4096]{1,0:T(8,128)(2,1)} %bitcast.2, bf16[16,32,128]{2,1,0:T(8,128)(2,1)} %alpha.1, bf16[2048,4096]{1,0:T(8,128)(2,1)} %basis_hbm.1, ...), custom_call_target="tpu_custom_call" | custom-call | tf_op jit(solution)/shard_map/pallas_call | solution.py:310
  75.1 1.9 %copy.12 = f32[32,4096]{1,0:T(8,128)} copy(f32[32,4096]{1,0:T(8,128)} %get-tuple-element.4) | data formatting | bytes 1048576
  77.0 1.7 %copy.13 = f32[16,32,128]{2,1,0:T(8,128)} copy(f32[16,32,128]{2,1,0:T(8,128)} %get-tuple-element.5) | data formatting | bytes 524288

commit v2 on v1

v2 whole, which is shorter than its diff:
```python
import functools

import jax
import jax.numpy as jnp
from jax import lax
from jax.experimental import pallas as pl
from jax.experimental.pallas import tpu as pltpu
from jax.sharding import PartitionSpec as P

MESH = pl.DeviceIdType.MESH
NT = (((1,), (1,)), ((), ()))
HIGH = lax.Precision.HIGHEST
F32 = jnp.float32
BF16 = jnp.bfloat16


def kernel(
    order, inverse, gains, anom_hbm, alpha, basis_hbm, grad, root, band,
    inc_out, ag_out,
    basis, anom, weighted, part, half, outgo, landed, rsend, rland, coefs, zall0, zall1, ypart, ysend,
    inc_acc, inc_send, inc_land, inc_own, inc_all, gall0, gall1, gpart, gsend,
    load_sem, asem, z_s, z_r, y_s, y_r, q_s, q_r, px_s, px_r, py_s, py_r, d_s, d_r, x_s, x_r,
    r_s, r_r, ry_s, ry_r, i_s, i_r, o_s, o_r, gz_s, gz_r, gy_s, gy_r,
):
    zall, gall = (zall0, zall1), (gall0, gall1)
    m = lax.axis_index("mem")
    s = lax.axis_index("state")
    z, yl = m // 2, m % 2
    chip, core = s // 2, s % 2
    yh, x = chip // 4, chip % 4
    other = 1 - core

    def chip_at(t):
        return ((yh + t // 4) % 2) * 4 + (x + t % 4) % 4

    def mem_at(u):
        return ((z + u // 2) % 4) * 2 + (yl + u % 2) % 2

    def back(t):
        return (t // 4) * 4 + (4 - t % 4) % 4

    def remote(src, dst, send, recv, mem, state):
        return pltpu.make_async_remote_copy(
            src_ref=src, dst_ref=dst, send_sem=send, recv_sem=recv,
            device_id=(mem, state), device_id_type=MESH,
        )

    def lanes(start, width):
        return pl.ds(pl.multiple_of(start, 128), width)

    partner = chip * 2 + other
    ymate = z * 2 + (1 - yl)

    def load(r):
        q = chip_at(7 - r)
        return pltpu.make_async_copy(
            basis_hbm.at[pl.ds(pl.multiple_of(q * 256, 256), 256), :],
            basis.at[pl.ds(pl.multiple_of(r * 256, 256), 256), :],
            load_sem.at[r],
        )

    def load_anom(g):
        rows = pl.ds(g * 128, 128)
        return pltpu.make_async_copy(anom_hbm.at[rows, :], anom.at[rows, :], asem.at[g])

    for g in range(4):
        load_anom(g).start()
    load(0).start()
    load(1).start()

    barrier = pltpu.get_barrier_semaphore()
    for u in range(1, 8):
        pl.semaphore_signal(barrier, inc=1, device_id=(mem_at(u), s), device_id_type=MESH)
    for t in range(1, 5):
        pl.semaphore_signal(
            barrier, inc=1, device_id=(m, chip_at(t) * 2 + core), device_id_type=MESH
        )
    pl.semaphore_signal(barrier, inc=1, device_id=(m, partner), device_id_type=MESH)

    bands = band[...]
    gain = jnp.zeros((1, 128), F32)
    for b in range(16):
        gain = jnp.where(bands == b, gains[b], gain)
    rooted = jnp.concatenate([root[...]] * 4, axis=0)
    rooted = jnp.concatenate([rooted] * 4, axis=1)
    row = lax.broadcasted_iota(jnp.int32, (128, 128), 0) // 32
    col = lax.broadcasted_iota(jnp.int32, (128, 128), 1) // 32
    rooted = jnp.where(row == col, rooted, 0.0)
    def spread(halves, g, value):
        value = value.astype(BF16).reshape(4, 32, 128)
        for h in range(2):
            halves[h][pl.ds(z * 16 + g * 4, 4)] = value[:, h * 16:(h + 1) * 16, :]

    for g in range(4):
        block = alpha[g * 4:(g + 1) * 4].astype(F32).reshape(128, 128)
        value = jnp.dot(rooted, block, precision=HIGH, preferred_element_type=F32) * gain
        spread(zall, g, value)

    with jax.named_scope('bar'):
        pl.semaphore_wait(barrier, 12)

    def z_copy(all_ref, h, dz, send, recv, got):
        mine = all_ref[h].at[pl.ds(z * 16, 16)]
        dst = all_ref[h].at[pl.ds(((z + 4 - dz) % 4) * 16, 16)] if got else mine
        k = h * 3 + dz - 1
        return remote(mine, dst, send.at[k], recv.at[k], ((z + dz) % 4) * 2 + yl, s)

    for h in range(2):
        for dz in (1, 3, 2):
            z_copy(zall, h, dz, z_s, z_r, False).start()

    for g in range(4):
        with jax.named_scope('anomwait'):
            load_anom(g).wait()

        def weigh(c, carry):
            w = lanes(c * 512, 512)
            factor = grad[:, w].astype(F32)
            for k in range(4):
                rows = pl.ds(g * 128 + k * 32, 32)
                weighted[rows, w] = (anom[rows, w].astype(F32) * factor).astype(BF16)
            return carry

        lax.fori_loop(0, 8, weigh, 0)

    def pick(table, all_ref, h, slot):
        where = table[slot]
        same = (where // 16) % 2 == yl
        return same, all_ref[h][(where // 32) * 16 + where % 16]

    def y_copy(src, dst, h, send, recv):
        levels = pl.ds(h * 16, 16)
        return remote(
            src.at[:, levels], dst.at[:, levels], send.at[h], recv.at[h], ymate, s
        )

    def exchange(table, all_ref, src, dst, h, zs, zr, ys, yr):
        for dz in (1, 3, 2):
            z_copy(all_ref, h, dz, zs, zr, True).wait_recv()
        for i in range(16):
            same, value = pick(table, all_ref, h, ymate * 16 + i)
            src[i, pl.ds(h * 16, 16), :] = jnp.where(same, value, jnp.zeros_like(value))
        y_copy(src, dst, h, ys, yr).start()

    def block(r, h, c):
        return coefs.at[:, pl.ds(h * 16, 16), lanes(r * 256 + c * 128, 128)]

    def b_copy(source, target, h, t, send, recv):
        return remote(
            block(source, h, core), block(target, h, core), send, recv,
            m, chip_at(t) * 2 + core,
        )

    def q_y():
        return b_copy(7, 3, 0, 4, q_s.at[0], q_r.at[0])

    def q_x(dx):
        return b_copy(7, 3 + dx, 0, dx, q_s.at[dx], q_r.at[4 - dx])

    def q_m(dx):
        return b_copy(3, dx - 1, 0, dx, q_s.at[3 + dx], q_r.at[7 - dx])

    def p_x(dx):
        return b_copy(7, 3 + dx, 1, dx, px_s.at[dx - 1], px_r.at[3 - dx])

    def p_y(dx):
        return b_copy(7 - dx, 3 - dx, 1, 4, py_s.at[dx], py_r.at[dx])

    def b_got(r, h, recv):
        here = block(r, h, core)
        return remote(here, here, q_s.at[0], recv, m, chip_at(4) * 2 + core)

    def d_copy(r, h):
        here = block(r, h, core)
        return remote(here, here, d_s.at[2 * r + h], d_r.at[2 * r + h], m, partner)

    def d_got(r, h):
        there = block(r, h, other)
        return remote(there, there, d_s.at[2 * r + h], d_r.at[2 * r + h], m, partner)

    def settle(h):
        y_copy(ysend, ypart, h, y_s, y_r).wait_recv()
        for i in range(16):
            same, value = pick(inverse, zall, h, m * 16 + i)
            coefs[i, pl.ds(h * 16, 16), lanes(7 * 256 + core * 128, 128)] = jnp.where(
                same, value, ypart[i, pl.ds(h * 16, 16), :]
            )

    def x_copy(r):
        return remote(
            part.at[r, :, lanes(other * 128, 128)], half.at[r], x_s.at[r], x_r.at[r], m, partner
        )

    def r_copy(r):
        return remote(
            outgo.at[r], landed.at[r], r_s.at[r], r_r.at[r], m,
            chip_at((7 - r) % 4) * 2 + core,
        )

    def ry_copy():
        return remote(rsend, rland, ry_s.at[0], ry_r.at[0], m, chip_at(4) * 2 + core)

    def own(r, rows):
        return part[r, rows, lanes(core * 128, 128)] + half[r, rows, :]

    def adjoint(r, carry):
        @pl.when(r < 6)
        def _():
            load(r + 2).start()

        with jax.named_scope('bwait'):
            load(r).wait()
        rows = pl.ds(pl.multiple_of(r * 256, 256), 256)
        with jax.named_scope('adot'):
            part[r] = lax.dot_general(weighted[...], basis[rows, :], NT, preferred_element_type=F32)
        x_copy(r).start()

        @pl.when(r > 0)
        def _():
            p = r - 1
            with jax.named_scope('xwait'):
                x_copy(p).wait_recv()

            @pl.when(p != 3)
            def _():
                outgo[p] = (part[p, :, lanes(core * 128, 128)] + half[p]).astype(BF16)
                r_copy(p).start()

        @pl.when(r == 2)
        def _():
            with jax.named_scope('zwait'):
                exchange(inverse, zall, ysend, ypart, 0, z_s, z_r, y_s, y_r)

        @pl.when(r == 4)
        def _():
            with jax.named_scope('zwait'):
                exchange(inverse, zall, ysend, ypart, 1, z_s, z_r, y_s, y_r)

        @pl.when(r == 5)
        def _():
            with jax.named_scope('ywait'):
                settle(0)
            q_y().start()
            for dx in (1, 3, 2):
                q_x(dx).start()

        @pl.when(r == 6)
        def _():
            with jax.named_scope('ywait'):
                settle(1)
            p_y(0).start()
            for dx in (1, 3, 2):
                p_x(dx).start()
            for h in range(2):
                d_copy(7, h).start()

        return carry

    lax.fori_loop(0, 8, adjoint, 0)

    with jax.named_scope('qywait'):
        b_got(3, 0, q_r.at[0]).wait_recv()
    for dx in (1, 3, 2):
        q_m(dx).start()
    d_copy(3, 0).start()

    for r in range(3):
        with jax.named_scope('rfwait'):
            r_copy(r).wait_recv()
    for g in range(4):
        rows = pl.ds(g * 128, 128)
        total = own(3, rows)
        for r in range(3):
            total = total + landed[r, rows, :].astype(F32)
        rsend[rows, :] = total
    ry_copy().start()

    for dx in (1, 3, 2):
        with jax.named_scope('qxwait'):
            b_got(7 - dx, 0, q_r.at[dx]).wait_recv()
        d_copy(7 - dx, 0).start()
    for dx in (1, 3, 2):
        with jax.named_scope('pxwait'):
            b_got(7 - dx, 1, px_r.at[dx - 1]).wait_recv()
        p_y(dx).start()
        d_copy(7 - dx, 1).start()

    def field_part(low, c):
        w = lanes(c * 512, 512)
        f = jnp.dot(
            coefs[:, :, low:low + 1024].reshape(512, 1024), basis[low:low + 1024, w],
            preferred_element_type=F32,
        )
        return w, jnp.sum((f * anom[:, w].astype(F32)).reshape(16, 32, 512), axis=0)

    for r in (7, 6, 4, 5):
        for h in range(2):
            with jax.named_scope('dwait'):
                d_got(r, h).wait_recv()

    def near(c, carry):
        with jax.named_scope('near'):
            w, value = field_part(1024, c)
        inc_acc[:, w] = value

        @pl.when(c == 1)
        def _():
            with jax.named_scope('rnwait'):
                x_copy(7).wait_recv()
                for r in range(4, 7):
                    r_copy(r).wait_recv()
                ry_copy().wait_recv()
            for g in range(4):
                rows = pl.ds(g * 128, 128)
                total = own(7, rows) + rland[rows, :]
                for r in range(4, 7):
                    total = total + landed[r, rows, :].astype(F32)
                value = jnp.dot(rooted.T, total, precision=HIGH, preferred_element_type=F32) * gain
                spread(gall, g, value)
            for h in range(2):
                for dz in (1, 3, 2):
                    z_copy(gall, h, dz, gz_s, gz_r, False).start()

        @pl.when(c == 4)
        def _():
            for dx in (1, 3, 2):
                with jax.named_scope('qmwait'):
                    b_got(3 - dx, 0, q_r.at[3 + dx]).wait_recv()
                d_copy(3 - dx, 0).start()
            for dx in (0, 1, 3, 2):
                with jax.named_scope('pywait'):
                    b_got(3 - dx, 1, py_r.at[dx]).wait_recv()
                d_copy(3 - dx, 1).start()

        return carry

    lax.fori_loop(0, 8, near, 0)

    for r in range(4):
        for h in range(2):
            with jax.named_scope('fdwait'):
                d_got(r, h).wait_recv()

    def i_copy(i):
        return remote(inc_send.at[i], inc_land.at[i], i_s.at[i], i_r.at[i], mem_at(7 - i), s)

    def far(i, carry):
        with jax.named_scope('far'):
            w, value = field_part(0, mem_at(7 - i))
        inc_send[i] = (value + inc_acc[:, w]).astype(BF16)

        @pl.when(i < 7)
        def _():
            i_copy(i).start()

        @pl.when(i == 2)
        def _():
            with jax.named_scope('gzwait'):
                exchange(order, gall, gsend, gpart, 0, gz_s, gz_r, gy_s, gy_r)

        @pl.when(i == 4)
        def _():
            with jax.named_scope('gzwait'):
                exchange(order, gall, gsend, gpart, 1, gz_s, gz_r, gy_s, gy_r)

        return carry

    lax.fori_loop(0, 8, far, 0)

    total = inc_send[7].astype(F32)
    for i in range(7):
        with jax.named_scope(f'iwait{i}'):
            i_copy(i).wait_recv()
        total = total + inc_land[i].astype(F32)
    inc_own[...] = total.astype(BF16)

    def o_copy(u, got):
        target = mem_at(u)
        spot = mem_at(((4 - u // 2) % 4) * 2 + u % 2) if got else m
        return remote(
            inc_own, inc_all.at[spot], o_s.at[u - 1], o_r.at[u - 1], target, s
        )

    for u in (4, 5, 1, 2, 3, 6, 7):
        o_copy(u, False).start()
    inc_out[:, lanes(m * 512, 512)] = inc_own[...].astype(F32)

    for h in range(2):
        with jax.named_scope('gywait'):
            y_copy(gsend, gpart, h, gy_s, gy_r).wait_recv()
        for i in range(16):
            same, value = pick(order, gall, h, m * 16 + i)
            levels = pl.ds(h * 16, 16)
            ag_out[i, levels, :] = jnp.where(same, value, gpart[i, levels, :]).astype(F32)

    for u in range(1, 8):
        with jax.named_scope('owait'):
            o_copy(u, True).wait_recv()
        spot = mem_at(((4 - u // 2) % 4) * 2 + u % 2)
        inc_out[:, lanes(spot * 512, 512)] = inc_all[spot].astype(F32)

    for h in range(2):
        for dz in (1, 2, 3):
            z_copy(zall, h, dz, z_s, z_r, False).wait_send()
            z_copy(gall, h, dz, gz_s, gz_r, False).wait_send()
        y_copy(ysend, ypart, h, y_s, y_r).wait_send()
        y_copy(gsend, gpart, h, gy_s, gy_r).wait_send()
    q_y().wait_send()
    p_y(0).wait_send()
    for dx in (1, 2, 3):
        q_x(dx).wait_send()
        q_m(dx).wait_send()
        p_x(dx).wait_send()
        p_y(dx).wait_send()
    for r in (0, 1, 2, 4, 5, 6):
        r_copy(r).wait_send()
    ry_copy().wait_send()
    for t in range(1, 8):
        i_copy(t - 1).wait_send()
        o_copy(t, False).wait_send()
    for r in range(8):
        x_copy(r).wait_send()
        for h in range(2):
            d_copy(r, h).wait_send()


def on_device(anomalies, alpha, basis, gradient, vertical_root, band_gain, band, order):
    members, levels, columns = anomalies.shape
    slots = jnp.arange(order.shape[0], dtype=jnp.int32)
    inverse = jnp.sum(jnp.where(order[None, :] == slots[:, None], slots[None, :], 0), axis=1)
    vmem, smem = pl.BlockSpec(memory_space=pltpu.VMEM), pl.BlockSpec(memory_space=pltpu.SMEM)
    hbm = pl.BlockSpec(memory_space=pl.ANY)
    dma = lambda n: pltpu.SemaphoreType.DMA((n,))
    return pl.pallas_call(
        kernel,
        out_shape=(
            jax.ShapeDtypeStruct((32, 4096), F32),
            jax.ShapeDtypeStruct((16, 32, 128), F32),
        ),
        in_specs=[smem, smem, smem, hbm, vmem, hbm, vmem, vmem, vmem],
        out_specs=(vmem, vmem),
        scratch_shapes=[
            pltpu.VMEM((2048, 4096), BF16),
            pltpu.VMEM((512, 4096), BF16),
            pltpu.VMEM((512, 4096), BF16),
            pltpu.VMEM((8, 512, 256), F32),
            pltpu.VMEM((8, 512, 128), F32),
            pltpu.VMEM((7, 512, 128), BF16),
            pltpu.VMEM((7, 512, 128), BF16),
            pltpu.VMEM((512, 128), F32),
            pltpu.VMEM((512, 128), F32),
            pltpu.VMEM((16, 32, 2048), BF16),
            pltpu.VMEM((64, 16, 128), BF16),
            pltpu.VMEM((64, 16, 128), BF16),
            pltpu.VMEM((16, 32, 128), BF16),
            pltpu.VMEM((16, 32, 128), BF16),
            pltpu.VMEM((32, 4096), F32),
            pltpu.VMEM((8, 32, 512), BF16),
            pltpu.VMEM((7, 32, 512), BF16),
            pltpu.VMEM((32, 512), BF16),
            pltpu.VMEM((8, 32, 512), BF16),
            pltpu.VMEM((64, 16, 128), BF16),
            pltpu.VMEM((64, 16, 128), BF16),
            pltpu.VMEM((16, 32, 128), BF16),
            pltpu.VMEM((16, 32, 128), BF16),
            dma(8), dma(4), dma(6), dma(6), dma(2), dma(2), dma(7), dma(7), dma(3), dma(3),
            dma(4), dma(4), dma(16), dma(16), dma(8), dma(8), dma(7), dma(7), dma(1), dma(1),
            dma(7), dma(7), dma(7), dma(7), dma(6), dma(6), dma(2), dma(2),
        ],
        compiler_params=pltpu.CompilerParams(
            collective_id=0, has_side_effects=True, vmem_limit_bytes=60 << 20
        ),
    )(
        order, inverse, band_gain, anomalies.reshape(members * levels, columns), alpha, basis,
        gradient, vertical_root, band.reshape(1, -1),
    )


def solution(mesh):
    return jax.shard_map(
        on_device,
        mesh=mesh,
        in_specs=(
            P("mem", None, "state"),
            P("mem", None, "state"),
            P(None, "state"),
            P(None, "state"),
            P(),
            P(),
            P("state"),
            P(),
        ),
        out_specs=(P(None, "state"), P("mem", None, "state")),
        check_vma=False,
    )
```

time: 78.9 us -> 61.5 us (0.78)
  the two profiles are of different devices: /device:TPU:0 before, /device:TPU:2 now
where the time goes in v2:
time: 61.5 us; the launch traced here: 61.3 us
  Pallas kernels  55.8 us (91%)
  local copies, waits for them, and re-layouts  3.54 us (6%)
  other arithmetic  1.28 us (2%)
  between operations  0.64 us (1%)
    pallas_call x1, Pallas kernels, on_device(): pl.pallas_call(kernel, out_shape=(jax.ShapeDtypeStruct((32, 4096), F32),...  55.8 us
    unnamed x2, local copies, waits for them, and re-layouts  3.54 us
    reduce_sum x1, other arithmetic, on_device(): jnp.sum(jnp.where(order[None, :] == slots[:, None], slots[None, :], 0), a...  1.28 us

profile of v2, /device:TPU:2, one launch (start us, length us, event | category | flops | bytes accessed | tf_op | source)
XLA Modules:
  0.0 61.3 jit_solution(5482708347380183008)
XLA Ops:
  0.6 1.3 %select_reduce_fusion.inverse = s32[128]{0:T(128)} fusion(s32[128]{0:T(128)} %order.1), kind=kLoop, calls=%fused_computation | loop fusion | flops 49024 | bytes 1024 | tf_op jit(solution)/shard_map/reduce_sum | solution.py:430
  1.9 55.8 %shard_map.95 = (f32[32,4096]{1,0:T(8,128)}, f32[16,32,128]{2,1,0:T(8,128)}) custom-call(s32[128]{0:T(128)} %order.1, s32[128]{0:T(128)} %select_reduce_fusion.inverse, f32[16]{0:T(128)} %gains.1, bf16[512,4096]{1,0:T(8,128)(2,1)} %bitcast.2, bf16[16,32,128]{2,1,0:T(8,128)(2,1)} %alpha.1, bf16[2048,4096]{1,0:T(8,128)(2,1)} %basis_hbm.1, ...), custom_call_target="tpu_custom_call" | custom-call | tf_op jit(solution)/shard_map/pallas_call | solution.py:434
  57.8 1.9 %copy.12 = f32[32,4096]{1,0:T(8,128)} copy(f32[32,4096]{1,0:T(8,128)} %get-tuple-element.4) | data formatting | bytes 1048576
  59.6 1.7 %copy.13 = f32[16,32,128]{2,1,0:T(8,128)} copy(f32[16,32,128]{2,1,0:T(8,128)} %get-tuple-element.5) | data formatting | bytes 524288

commit v3 on v2

v3 whole, which is shorter than its diff:
```python
import jax
import jax.numpy as jnp
from jax import lax
from jax.experimental import pallas as pl
from jax.experimental.pallas import tpu as pltpu
from jax.sharding import PartitionSpec as P

MESH = pl.DeviceIdType.MESH
NT = (((1,), (1,)), ((), ()))
HIGH = lax.Precision.HIGHEST
F32 = jnp.float32
BF16 = jnp.bfloat16
scope = jax.named_scope


def kernel(
    order_hbm, gains_hbm, anom_hbm, alpha_hbm, basis_hbm, grad_hbm, root_hbm, band_hbm,
    inc_out, ag_out,
    order_v, order, inverse_v, inverse, gains, alpha, grad, root, band,
    basis, anom, weighted, part, half, outgo, landed, rsend, rland, coefs0, coefs1,
    zall0, zall1, ypart, ysend, inc_acc, inc_send, inc_land, inc_own, inc_all, gall0, gall1, gpart, gsend,
    small_sem, load_sem, asem, z_s, z_r, y_s, y_r, b_s, mate_r, row_r, rest_r, d_s, d_r, x_s, x_r,
    r_s, r_r, ry_s, ry_r, i_s, i_r, o_s, o_r, gz_s, gz_r, gy_s, gy_r,
):
    zall, gall, coefs = (zall0, zall1), (gall0, gall1), (coefs0, coefs1)
    m = lax.axis_index("mem")
    s = lax.axis_index("state")
    z, yl = m // 2, m % 2
    chip, core = s // 2, s % 2
    yh, x = chip // 4, chip % 4
    other = 1 - core

    def chip_at(t):
        return ((yh + t // 4) % 2) * 4 + (x + t % 4) % 4

    def mem_at(u):
        return ((z + u // 2) % 4) * 2 + (yl + u % 2) % 2

    def remote(src, dst, send, recv, mem, state):
        return pltpu.make_async_remote_copy(
            src_ref=src, dst_ref=dst, send_sem=send, recv_sem=recv,
            device_id=(mem, state), device_id_type=MESH,
        )

    def wait_all(ref, sem):
        pltpu.make_async_copy(ref, ref, sem).wait()

    def lanes(start, width):
        return pl.ds(pl.multiple_of(start, 128), width)

    partner = chip * 2 + other
    ymate = z * 2 + (1 - yl)

    barrier = pltpu.get_barrier_semaphore()
    for u in range(1, 8):
        pl.semaphore_signal(barrier, inc=1, device_id=(mem_at(u), s), device_id_type=MESH)
    for t in range(1, 5):
        pl.semaphore_signal(
            barrier, inc=1, device_id=(m, chip_at(t) * 2 + core), device_id_type=MESH
        )
    pl.semaphore_signal(barrier, inc=1, device_id=(m, partner), device_id_type=MESH)

    def small(k):
        source, target = (
            (alpha_hbm, alpha), (root_hbm, root), (band_hbm, band), (gains_hbm, gains),
            (order_hbm, order_v), (order_hbm, order), (grad_hbm, grad),
        )[k]
        return pltpu.make_async_copy(source, target, small_sem.at[k])

    def load(r):
        q = chip_at(7 - r)
        return pltpu.make_async_copy(
            basis_hbm.at[pl.ds(pl.multiple_of(q * 256, 256), 256), :],
            basis.at[pl.ds(pl.multiple_of(r * 256, 256), 256), :],
            load_sem.at[r],
        )

    def load_anom(g):
        group = pl.ds(g * 4, 4)
        return pltpu.make_async_copy(anom_hbm.at[group], anom.at[group], asem.at[g])

    for k in range(7):
        small(k).start()
    for g in range(4):
        load_anom(g).start()
    load(0).start()
    load(1).start()
    for k in range(6):
        small(k).wait()

    bands = band[...]
    gain = jnp.zeros((1, 128), F32)
    for b in range(16):
        gain = jnp.where(bands == b, gains[0, b], gain)
    rooted = jnp.concatenate([root[...]] * 4, axis=0)
    rooted = jnp.concatenate([rooted] * 4, axis=1)
    row = lax.broadcasted_iota(jnp.int32, (128, 128), 0)
    col = lax.broadcasted_iota(jnp.int32, (128, 128), 1)
    rooted = jnp.where(row // 32 == col // 32, rooted, 0.0)

    def spread(halves, g, value):
        value = value.astype(BF16).reshape(4, 32, 128)
        for h in range(2):
            halves[h][pl.ds(z * 16 + g * 4, 4)] = value[:, h * 16:(h + 1) * 16, :]

    for g in range(4):
        rows = alpha[g * 4:(g + 1) * 4].astype(F32).reshape(128, 128)
        value = jnp.dot(rooted, rows, precision=HIGH, preferred_element_type=F32) * gain
        spread(zall, g, value)

    held = (order_v[...] == row).astype(F32).astype(BF16)
    slots = lax.broadcasted_iota(jnp.int32, (8, 128), 1).astype(F32).astype(BF16)
    inverse_v[...] = lax.dot_general(slots, held, NT, preferred_element_type=F32).astype(jnp.int32)
    to_scalars = pltpu.make_async_copy(inverse_v, inverse, small_sem.at[7])
    to_scalars.start()

    with scope("bar"):
        pl.semaphore_wait(barrier, 12)

    def z_copy(all_ref, h, dz, send, recv):
        mine = all_ref[h].at[pl.ds(z * 16, 16)]
        return remote(mine, mine, send.at[h], recv.at[h], ((z + dz) % 4) * 2 + yl, s)

    for dz in (2, 1, 3):
        z_copy(zall, 0, dz, z_s, z_r).start()
    to_scalars.wait()

    small(6).wait()
    for g in range(4):
        with scope("anomwait"):
            load_anom(g).wait()

        def weigh(c, carry):
            w = lanes(c * 512, 512)
            factor = grad[:, w].astype(F32)
            for k in range(4):
                value = (anom[g * 4 + k, :, w].astype(F32) * factor).astype(BF16)
                weighted[pl.ds(g * 128 + k * 32, 32), w] = value
            return carry

        lax.fori_loop(0, 8, weigh, 0)
        if g == 1:
            for dz in (2, 1, 3):
                z_copy(zall, 1, dz, z_s, z_r).start()

    def pick(table, all_ref, h, slot):
        where = jnp.bitwise_and(table[0, slot], 127)
        same = (where // 16) % 2 == yl
        return same, all_ref[h][(where // 32) * 16 + where % 16]

    def y_copy(src, dst, h, send, recv):
        levels = pl.ds(h * 16, 16)
        return remote(
            src.at[:, levels], dst.at[:, levels], send.at[h], recv.at[h], ymate, s
        )

    def exchange(table, all_ref, src, dst, h, zs, zr, ys, yr):
        wait_all(all_ref[h].at[pl.ds(0, 48)], zr.at[h])
        for i in range(16):
            same, value = pick(table, all_ref, h, ymate * 16 + i)
            src[i, pl.ds(h * 16, 16), :] = jnp.where(same, value, jnp.zeros_like(value))
        y_copy(src, dst, h, ys, yr).start()

    def piece(h, e, r, c):
        return coefs[h].at[pl.ds(e * 8, 8), :, lanes(r * 256 + c * 128, 128)]

    def b_copy(h, e, source, target, t, recv):
        return remote(
            piece(h, e, source, core), piece(h, e, target, core), b_s.at[0], recv.at[h],
            m, chip_at(t) * 2 + core,
        )

    def d_copy(h, e, r):
        here = piece(h, e, r, core)
        return remote(here, here, d_s.at[0], d_r.at[2 * h + r // 4], m, partner)

    def settle(h):
        y_copy(ysend, ypart, h, y_s, y_r).wait_recv()
        for i in range(16):
            same, value = pick(inverse, zall, h, m * 16 + i)
            coefs[h][i, :, lanes(7 * 256 + core * 128, 128)] = jnp.where(
                same, value, ypart[i, pl.ds(h * 16, 16), :]
            )

    def launch(h):
        b_copy(h, 0, 7, 3, 4, mate_r).start()
        for dx in (2, 1, 3):
            for e in range(2):
                b_copy(h, e, 7, 3 + dx, dx, row_r).start()
        b_copy(h, 1, 7, 3, 4, rest_r).start()
        for e in range(2):
            d_copy(h, e, 7).start()

    def relay_mate(h):
        wait_all(coefs[h].at[pl.ds(0, 8), :, pl.ds(0, 128)], mate_r.at[h])
        for dx in (2, 1, 3):
            b_copy(h, 0, 3, dx - 1, dx, rest_r).start()
        d_copy(h, 0, 3).start()

    def relay_row(h):
        wait_all(coefs[h].at[pl.ds(0, 3)], row_r.at[h])
        for dx in (1, 3, 2):
            b_copy(h, 1, 7 - dx, 3 - dx, 4, rest_r).start()
            for e in range(2):
                d_copy(h, e, 7 - dx).start()

    def relay_rest(h):
        wait_all(coefs[h].at[pl.ds(0, 7), :, pl.ds(0, 1024)], rest_r.at[h])
        for r in range(3):
            for e in range(2):
                d_copy(h, e, r).start()
        d_copy(h, 1, 3).start()

    def gathered(h, far):
        wait_all(coefs[h].at[pl.ds(0, 4)], d_r.at[2 * h + 1 - far])

    def x_copy(r):
        return remote(
            part.at[r, :, lanes(other * 128, 128)], half.at[r], x_s.at[0], x_r.at[r], m, partner
        )

    def r_copy(r):
        return remote(
            outgo.at[r], landed.at[r], r_s.at[0], r_r.at[r // 4], m,
            chip_at((7 - r) % 4) * 2 + core,
        )

    def ry_copy():
        return remote(rsend, rland, ry_s.at[0], ry_r.at[0], m, chip_at(4) * 2 + core)

    def own(r, rows):
        return part[r, rows, lanes(core * 128, 128)] + half[r, rows, :]

    def adjoint(r, carry):
        @pl.when(r < 6)
        def _():
            load(r + 2).start()

        with scope("bwait"):
            load(r).wait()
        rows = pl.ds(pl.multiple_of(r * 256, 256), 256)
        with scope("adot"):
            part[r] = lax.dot_general(weighted[...], basis[rows, :], NT, preferred_element_type=F32)
        x_copy(r).start()

        @pl.when(r > 0)
        def _():
            p = r - 1
            with scope("xwait"):
                x_copy(p).wait_recv()

            @pl.when(p != 3)
            def _():
                outgo[p] = (part[p, :, lanes(core * 128, 128)] + half[p]).astype(BF16)

            @pl.when(p < 3)
            def _():
                r_copy(p).start()

        @pl.when(r == 2)
        def _():
            with scope("z0wait"):
                exchange(inverse, zall, ysend, ypart, 0, z_s, z_r, y_s, y_r)

        @pl.when(r == 4)
        def _():
            with scope("z1wait"):
                exchange(inverse, zall, ysend, ypart, 1, z_s, z_r, y_s, y_r)
            with scope("y0wait"):
                settle(0)
            launch(0)

        @pl.when(r == 6)
        def _():
            with scope("y1wait"):
                settle(1)
            launch(1)

        return carry

    lax.fori_loop(0, 8, adjoint, 0)

    with scope("mate0wait"):
        relay_mate(0)
    with scope("row0wait"):
        relay_row(0)
    for r in range(4, 7):
        r_copy(r).start()

    with scope("rfwait"):
        wait_all(landed.at[pl.ds(0, 3)], r_r.at[0])
    for g in range(4):
        rows = pl.ds(g * 128, 128)
        total = own(3, rows)
        for r in range(3):
            total = total + landed[r, rows, :].astype(F32)
        rsend[rows, :] = total
    ry_copy().start()

    def i_copy(h, i):
        return remote(
            inc_send.at[h, i], inc_land.at[h, i], i_s.at[0], i_r.at[h], mem_at(7 - i), s
        )

    def o_copy(h, u):
        return remote(
            inc_own.at[h], inc_all.at[h, m], o_s.at[0], o_r.at[h], mem_at(u), s
        )

    def field(h, low, w):
        with scope("field"):
            f = jnp.dot(
                coefs[h][:, :, low:low + 1024].reshape(256, 1024), basis[low:low + 1024, w],
                preferred_element_type=F32,
            )
            levels = pl.ds(h * 16, 16)
            product = f.reshape(16, 16, 512) * anom[:, levels, w].astype(F32)
            return jnp.sum(product, axis=0)

    def near(h, i):
        w = lanes(i * 512, 512)
        inc_acc[h, :, w] = field(h, 1024, w)

    def far(h, i):
        w = lanes(mem_at(7 - i) * 512, 512)
        inc_send[h, i] = (field(h, 0, w) + inc_acc[h, :, w]).astype(BF16)

        @pl.when(i < 7)
        def _():
            i_copy(h, i).start()

    def reduce_own(h):
        total = inc_send[h, 7].astype(F32)
        wait_all(inc_land.at[h], i_r.at[h])
        for i in range(7):
            total = total + inc_land[h, i].astype(F32)
        inc_own[h] = total.astype(BF16)
        for u in (4, 5, 1, 2, 3, 6, 7):
            o_copy(h, u).start()

    def near0(i, carry):
        near(0, i)

        @pl.when(i == 3)
        def _():
            with scope("mate1wait"):
                relay_mate(1)

        @pl.when(i == 6)
        def _():
            with scope("rest0wait"):
                relay_rest(0)

        return carry

    def far0(i, carry):
        far(0, i)

        @pl.when(i == 1)
        def _():
            with scope("row1wait"):
                relay_row(1)

        return carry

    def near1(i, carry):
        near(1, i)

        @pl.when(i == 4)
        def _():
            with scope("rest1wait"):
                relay_rest(1)

        @pl.when(i == 1)
        def _():
            with scope("rnwait"):
                x_copy(7).wait_recv()
                wait_all(landed.at[pl.ds(4, 3)], r_r.at[1])
                ry_copy().wait_recv()
            for g in range(4):
                rows = pl.ds(g * 128, 128)
                total = own(7, rows) + rland[rows, :]
                for r in range(4, 7):
                    total = total + landed[r, rows, :].astype(F32)
                value = jnp.dot(rooted.T, total, precision=HIGH, preferred_element_type=F32) * gain
                spread(gall, g, value)
            for h in range(2):
                for dz in (2, 1, 3):
                    z_copy(gall, h, dz, gz_s, gz_r).start()

        return carry

    def far1(i, carry):
        far(1, i)

        @pl.when(i == 1)
        def _():
            with scope("i0wait"):
                reduce_own(0)

        @pl.when(i == 5)
        def _():
            with scope("gz0wait"):
                exchange(order, gall, gsend, gpart, 0, gz_s, gz_r, gy_s, gy_r)

        return carry

    with scope("dn0wait"):
        gathered(0, False)
    lax.fori_loop(0, 8, near0, 0)
    with scope("df0wait"):
        gathered(0, True)
    lax.fori_loop(0, 8, far0, 0)
    with scope("dn1wait"):
        gathered(1, False)
    lax.fori_loop(0, 8, near1, 0)
    with scope("df1wait"):
        gathered(1, True)
    lax.fori_loop(0, 8, far1, 0)

    with scope("i1wait"):
        reduce_own(1)
    with scope("gz1wait"):
        exchange(order, gall, gsend, gpart, 1, gz_s, gz_r, gy_s, gy_r)

    for h in range(2):
        with scope("gywait"):
            y_copy(gsend, gpart, h, gy_s, gy_r).wait_recv()
        for i in range(16):
            same, value = pick(order, gall, h, m * 16 + i)
            levels = pl.ds(h * 16, 16)
            ag_out[i, levels, :] = jnp.where(same, value, gpart[i, levels, :]).astype(F32)

    for h in range(2):
        levels = pl.ds(h * 16, 16)
        inc_out[levels, lanes(m * 512, 512)] = inc_own[h].astype(F32)
        with scope("owait"):
            wait_all(inc_all.at[h, pl.ds(0, 7)], o_r.at[h])
        for u in range(1, 8):
            spot = mem_at(u)
            inc_out[levels, lanes(spot * 512, 512)] = inc_all[h, spot].astype(F32)

    with scope("sentwait"):
        for h in range(2):
            wait_all(zall[h].at[pl.ds(0, 48)], z_s.at[h])
            wait_all(gall[h].at[pl.ds(0, 48)], gz_s.at[h])
            y_copy(ysend, ypart, h, y_s, y_r).wait_send()
            y_copy(gsend, gpart, h, gy_s, gy_r).wait_send()
        wait_all(coefs0.at[pl.ds(0, 14)], b_s.at[0])
        wait_all(coefs0, d_s.at[0])
        wait_all(inc_land, i_s.at[0])
        wait_all(inc_land, o_s.at[0])
        wait_all(outgo.at[pl.ds(0, 6)], r_s.at[0])
        wait_all(half, x_s.at[0])
        ry_copy().wait_send()


def on_device(anomalies, alpha, basis, gradient, vertical_root, band_gain, band, order):
    vmem = pl.BlockSpec(memory_space=pltpu.VMEM)
    hbm = pl.BlockSpec(memory_space=pl.ANY)
    dma = lambda n: pltpu.SemaphoreType.DMA((n,))
    int32 = jnp.int32
    return pl.pallas_call(
        kernel,
        out_shape=(
            pltpu.VMEM((32, 4096), F32),
            pltpu.VMEM((16, 32, 128), F32),
        ),
        in_specs=[hbm] * 8,
        out_specs=(vmem, vmem),
        scratch_shapes=[
            pltpu.VMEM((1, 128), int32),
            pltpu.SMEM((1, 128), int32),
            pltpu.VMEM((8, 128), int32),
            pltpu.SMEM((8, 128), int32),
            pltpu.SMEM((1, 16), F32),
            pltpu.VMEM((16, 32, 128), BF16),
            pltpu.VMEM((32, 4096), BF16),
            pltpu.VMEM((32, 32), F32),
            pltpu.VMEM((1, 128), int32),
            pltpu.VMEM((2048, 4096), BF16),
            pltpu.VMEM((16, 32, 4096), BF16),
            pltpu.VMEM((512, 4096), BF16),
            pltpu.VMEM((8, 512, 256), F32),
            pltpu.VMEM((8, 512, 128), F32),
            pltpu.VMEM((7, 512, 128), BF16),
            pltpu.VMEM((7, 512, 128), BF16),
            pltpu.VMEM((512, 128), F32),
            pltpu.VMEM((512, 128), F32),
            pltpu.VMEM((16, 16, 2048), BF16),
            pltpu.VMEM((16, 16, 2048), BF16),
            pltpu.VMEM((64, 16, 128), BF16),
            pltpu.VMEM((64, 16, 128), BF16),
            pltpu.VMEM((16, 32, 128), BF16),
            pltpu.VMEM((16, 32, 128), BF16),
            pltpu.VMEM((2, 16, 4096), F32),
            pltpu.VMEM((2, 8, 16, 512), BF16),
            pltpu.VMEM((2, 7, 16, 512), BF16),
            pltpu.VMEM((2, 16, 512), BF16),
            pltpu.VMEM((2, 8, 16, 512), BF16),
            pltpu.VMEM((64, 16, 128), BF16),
            pltpu.VMEM((64, 16, 128), BF16),
            pltpu.VMEM((16, 32, 128), BF16),
            pltpu.VMEM((16, 32, 128), BF16),
            dma(8), dma(8), dma(4), dma(2), dma(2), dma(2), dma(2), dma(1), dma(2), dma(2), dma(2),
            dma(1), dma(4), dma(1), dma(8), dma(1), dma(2), dma(1), dma(1), dma(1), dma(2),
            dma(1), dma(2), dma(2), dma(2), dma(2), dma(2),
        ],
        compiler_params=pltpu.CompilerParams(
            collective_id=0, has_side_effects=True, vmem_limit_bytes=60 << 20
        ),
    )(
        order.reshape(1, -1), band_gain.reshape(1, -1), anomalies, alpha, basis, gradient,
        vertical_root, band.reshape(1, -1),
    )


def solution(mesh):
    return jax.shard_map(
        on_device,
        mesh=mesh,
        in_specs=(
            P("mem", None, "state"),
            P("mem", None, "state"),
            P(None, "state"),
            P(None, "state"),
            P(),
            P(),
            P("state"),
            P(),
        ),
        out_specs=(P(None, "state"), P("mem", None, "state")),
        check_vma=False,
    )
```

time: 61.5 us -> 56 us (0.911)
  the two profiles are of different devices: /device:TPU:2 before, /device:TPU:0 now
where the time goes in v3:
time: 56 us; the launch traced here: 55.5 us
  Pallas kernels  53.4 us (95%)
  local copies, waits for them, and re-layouts  1.5 us (3%)
  between operations  0.64 us (1%)
    pallas_call x1, Pallas kernels, on_device(): pl.pallas_call(kernel, out_shape=(pltpu.VMEM((32, 4096), F32), pltpu.VMEM...  53.4 us
    unnamed x2, local copies, waits for them, and re-layouts  1.5 us

profile of v3, /device:TPU:0, one launch (start us, length us, event | category | flops | bytes accessed | tf_op | source)
XLA Modules:
  0.0 55.5 jit_solution(11781277892960684989)
XLA Ops:
  0.6 53.4 %shard_map.95 = (f32[32,4096]{1,0:T(8,128)S(1)}, f32[16,32,128]{2,1,0:T(8,128)S(1)}) custom-call(s32[1,128]{1,0:T(1,128)} %bitcast.3, f32[1,16]{1,0:T(1,128)} %bitcast.4, bf16[16,32,4096]{2,1,0:T(8,128)(2,1)} %anom_hbm.1, bf16[16,32,128]{2,1,0:T(8,128)(2,1)} %alpha_hbm.1, bf16[2048,4096]{1,0:T(8,128)(2,1)} %basis_hbm.1, bf16[32,4096]{1,0:T(8,128)(2,1)} %grad_hbm.1, ...), custom_call_target="tpu_custom_call" | custom-call | tf_op jit(solution)/shard_map/pallas_call | solution.py:463
  54.0 0.8 %copy.12 = f32[32,4096]{1,0:T(8,128)} copy(f32[32,4096]{1,0:T(8,128)S(1)} %get-tuple-element.2) | data formatting | bytes 1048576
  54.8 0.7 %copy.13 = f32[16,32,128]{2,1,0:T(8,128)} copy(f32[16,32,128]{2,1,0:T(8,128)S(1)} %get-tuple-element.3) | data formatting | bytes 524288

commit v4 on v3

v4 whole, which is shorter than its diff:
```python
import jax
import jax.numpy as jnp
from jax import lax
from jax.experimental import pallas as pl
from jax.experimental.pallas import tpu as pltpu
from jax.sharding import PartitionSpec as P

MESH = pl.DeviceIdType.MESH
NT = (((1,), (1,)), ((), ()))
HIGH = lax.Precision.HIGHEST
F32 = jnp.float32
BF16 = jnp.bfloat16
scope = jax.named_scope


def kernel(
    order_hbm, gains_hbm, anom_hbm, alpha_hbm, basis_hbm, grad_hbm, root_hbm, band_hbm,
    inc_out, ag_out,
    order_v, order, inverse_v, inverse, gains, alpha, grad, root, band,
    basis, anom, weighted, part, half, outgo, relayed, landed, rsend, rland, coefs0, coefs1,
    zall, ypart, ysend, zpair, zout, zland, inc_acc, inc_send, inc_land, inc_own, inc_all, gall, gpart, gsend, gpair, gout, gland,
    small_sem, load_sem, asem, z_s, z_r, b_s, mate_r, row_r, rest_r, d_s, d_r, x_s, x_r,
    rd_s, rd_r, r_s, r_r, ry_s, ry_r, i_s, i_r, o_s, o_r, gz_s, gz_r,
):
    coefs = (coefs0, coefs1)
    m = lax.axis_index("mem")
    s = lax.axis_index("state")
    z, yl = m // 2, m % 2
    chip, core = s // 2, s % 2
    yh, x = chip // 4, chip % 4
    other = 1 - core

    def chip_at(t):
        return ((yh + t // 4) % 2) * 4 + (x + t % 4) % 4

    def mem_at(u):
        return ((z + u // 2) % 4) * 2 + (yl + u % 2) % 2

    def remote(src, dst, send, recv, mem, state):
        return pltpu.make_async_remote_copy(
            src_ref=src, dst_ref=dst, send_sem=send, recv_sem=recv,
            device_id=(mem, state), device_id_type=MESH,
        )

    def wait_all(ref, sem):
        pltpu.make_async_copy(ref, ref, sem).wait()

    def lanes(start, width):
        return pl.ds(pl.multiple_of(start, 128), width)

    partner = chip * 2 + other
    ymate = z * 2 + (1 - yl)

    barrier = pltpu.get_barrier_semaphore()
    for u in range(1, 8):
        pl.semaphore_signal(barrier, inc=1, device_id=(mem_at(u), s), device_id_type=MESH)
    for t in range(1, 5):
        pl.semaphore_signal(
            barrier, inc=1, device_id=(m, chip_at(t) * 2 + core), device_id_type=MESH
        )
    pl.semaphore_signal(barrier, inc=1, device_id=(m, partner), device_id_type=MESH)

    def small(k):
        source, target = (
            (alpha_hbm, alpha), (root_hbm, root), (band_hbm, band), (gains_hbm, gains),
            (order_hbm, order_v), (order_hbm, order), (grad_hbm, grad),
        )[k]
        return pltpu.make_async_copy(source, target, small_sem.at[k])

    def slot_at(r):
        a, b = (r % 4) // 2, r % 2
        return (r // 4) * 4 + 3 - (2 + a - b * (1 + 2 * a))

    def load(r):
        slot = slot_at(r)
        q = chip_at(7 - slot)
        return pltpu.make_async_copy(
            basis_hbm.at[pl.ds(pl.multiple_of(q * 256, 256), 256), :],
            basis.at[pl.ds(pl.multiple_of(slot * 256, 256), 256), :],
            load_sem.at[r],
        )

    def load_anom(g):
        group = pl.ds(g * 4, 4)
        return pltpu.make_async_copy(anom_hbm.at[group], anom.at[group], asem.at[g])

    for k in range(7):
        small(k).start()
    for g in range(4):
        load_anom(g).start()
    load(0).start()
    with scope("smallwait"):
        for k in range(6):
            small(k).wait()

    bands = band[...]
    gain = jnp.zeros((1, 128), F32)
    for b in range(16):
        gain = jnp.where(bands == b, gains[0, b], gain)
    rooted = jnp.concatenate([root[...]] * 4, axis=0)
    rooted = jnp.concatenate([rooted] * 4, axis=1)
    row = lax.broadcasted_iota(jnp.int32, (128, 128), 0)
    col = lax.broadcasted_iota(jnp.int32, (128, 128), 1)
    rooted = jnp.where(row // 32 == col // 32, rooted, 0.0)

    def spread(all_ref, pair, g, value):
        value = value.astype(BF16).reshape(4, 32, 128)
        all_ref[pl.ds(z * 16 + g * 4, 4)] = value[:, :16, :]
        pair[pl.ds(yl * 16 + g * 4, 4)] = value[:, 16:, :]

    for g in range(4):
        rows = alpha[g * 4:(g + 1) * 4].astype(F32).reshape(128, 128)
        value = jnp.dot(rooted, rows, precision=HIGH, preferred_element_type=F32) * gain
        spread(zall, zpair, g, value)

    held = (order_v[...] == row).astype(F32).astype(BF16)
    slots = lax.broadcasted_iota(jnp.int32, (8, 128), 1).astype(F32).astype(BF16)
    inverse_v[...] = lax.dot_general(slots, held, NT, preferred_element_type=F32).astype(jnp.int32)
    to_scalars = pltpu.make_async_copy(inverse_v, inverse, small_sem.at[7])
    to_scalars.start()

    with scope("bar"):
        pl.semaphore_wait(barrier, 12)

    def z_copy(all_ref, dz, send, recv):
        mine = all_ref.at[pl.ds(z * 16, 16)]
        return remote(mine, mine, send.at[0], recv.at[0], ((z + dz) % 4) * 2 + yl, s)

    def y_copy(src, dst, send, recv):
        return remote(src, dst, send.at[1], recv.at[1], ymate, s)

    def pair_copy(pair, send, recv):
        mine = pair.at[pl.ds(yl * 16, 16)]
        return remote(mine, mine, send.at[2], recv.at[2], ymate, s)

    def out_copy(out, land, dz, send, recv):
        return remote(
            out.at[dz - 1], land.at[pl.ds(z * 16, 16)], send.at[3], recv.at[3],
            ((z + dz) % 4) * 2 + yl, s,
        )

    def depart(all_ref, pair, send, recv):
        for dz in (2, 1, 3):
            z_copy(all_ref, dz, send, recv).start()
        pair_copy(pair, send, recv).start()

    depart(zall, zpair, z_s, z_r)
    to_scalars.wait()

    small(6).wait()
    for g in range(4):
        with scope("anomwait"):
            load_anom(g).wait()
        if g == 1:
            load(1).start()

        def weigh(c, carry):
            w = lanes(c * 512, 512)
            factor = grad[:, w].astype(F32)
            for k in range(4):
                value = (anom[g * 4 + k, :, w].astype(F32) * factor).astype(BF16)
                weighted[pl.ds(g * 128 + k * 32, 32), w] = value
            return carry

        lax.fori_loop(0, 8, weigh, 0)

    def held_at(table, slot):
        return jnp.bitwise_and(table[0, slot], 127)

    def gathered_row(all_ref, where):
        return all_ref[(where // 32) * 16 + where % 16]

    def to_mate(table, all_ref, src, dst, send, recv):
        wait_all(all_ref.at[pl.ds(0, 48)], recv.at[0])
        for i in range(16):
            src[i] = gathered_row(all_ref, held_at(table, ymate * 16 + i))
        y_copy(src, dst, send, recv).start()

    def to_z(table, pair, out, land, send, recv):
        pair_copy(pair, send, recv).wait_recv()
        for dz in (2, 1, 3):
            for i in range(16):
                where = held_at(table, (((z + dz) % 4) * 2 + yl) * 16 + i)
                out[dz - 1, i] = pair[where % 32]
            out_copy(out, land, dz, send, recv).start()
        for i in range(16):
            land[z * 16 + i] = pair[held_at(table, m * 16 + i) % 32]

    def arrived(table, h, all_ref, src, dst, land, send, recv):
        if h:
            wait_all(land.at[pl.ds(0, 48)], recv.at[3])
        else:
            y_copy(src, dst, send, recv).wait_recv()
        for i in range(16):
            where = held_at(table, m * 16 + i)
            if h:
                yield i, land[(where // 32) * 16 + i]
            else:
                same = (where // 16) % 2 == yl
                yield i, jnp.where(same, gathered_row(all_ref, where), dst[i])

    def parts(h):
        return (0, 1) if h == 0 else (0,)

    def piece(h, e, r, c):
        count = 16 // len(parts(h))
        return coefs[h].at[pl.ds(e * count, count), :, lanes(r * 256 + c * 128, 128)]

    def b_copy(h, e, source, target, t, recv):
        return remote(
            piece(h, e, source, core), piece(h, e, target, core), b_s.at[0], recv.at[h],
            m, chip_at(t) * 2 + core,
        )

    def d_copy(h, e, r):
        here = piece(h, e, r, core)
        return remote(here, here, d_s.at[0], d_r.at[2 * h + r // 4], m, partner)

    def settle(h):
        for i, value in arrived(inverse, h, zall, ysend, ypart, zland, z_s, z_r):
            coefs[h][i, :, lanes(7 * 256 + core * 128, 128)] = value

    def launch_y(h):
        b_copy(h, 0, 7, 3, 4, mate_r).start()
        if h == 0:
            b_copy(h, 1, 7, 3, 4, rest_r).start()
        for e in parts(h):
            d_copy(h, e, 7).start()

    def launch_x(h):
        for dx in (2, 1, 3):
            for e in parts(h):
                b_copy(h, e, 7, 3 + dx, dx, row_r).start()

    def relay_mate(h):
        wait_all(piece(h, 0, 3, core), mate_r.at[h])
        for dx in (2, 1, 3):
            b_copy(h, 0, 3, dx - 1, dx, rest_r).start()
        d_copy(h, 0, 3).start()

    def relay_row(h):
        wait_all(coefs[h].at[pl.ds(0, 3)], row_r.at[h])
        for dx in (1, 3, 2):
            if h == 0:
                b_copy(h, 1, 7 - dx, 3 - dx, 4, rest_r).start()
            for e in parts(h):
                d_copy(h, e, 7 - dx).start()

    def relay_rest(h):
        if h == 0:
            wait_all(coefs[h].at[pl.ds(0, 7), :, pl.ds(0, 1024)], rest_r.at[h])
            d_copy(h, 1, 3).start()
        else:
            wait_all(coefs[h].at[pl.ds(0, 3)], rest_r.at[h])
        for r in range(3):
            for e in parts(h):
                d_copy(h, e, r).start()

    def gathered(h, far):
        wait_all(coefs[h].at[pl.ds(0, 4)], d_r.at[2 * h + 1 - far])

    def x_copy(r):
        return remote(
            part.at[r, :, lanes(other * 128, 128)], half.at[r], x_s.at[0], x_r.at[r], m, partner
        )

    def rd_copy(g, side):
        rows = pl.ds(side * 256, 256)
        return remote(
            outgo.at[4 * g + 1, rows], relayed.at[g, rows], rd_s.at[0], rd_r.at[g], m,
            chip_at(1 + 2 * side) * 2 + core,
        )

    def r_copy(g, side):
        slot = 4 * g + 2 - 2 * side
        return remote(
            outgo.at[slot], landed.at[g, side], r_s.at[0], r_r.at[g], m,
            chip_at(1 + 2 * side) * 2 + core,
        )

    def pass_half(g):
        slot = 4 * g + 1
        outgo[slot] = own(slot, pl.ds(0, 512)).astype(BF16)
        for side in range(2):
            rd_copy(g, side).start()

    def combine(g):
        wait_all(relayed.at[g], rd_r.at[g])
        for side in range(2):
            slot = 4 * g + 2 - 2 * side
            for part_side in range(2):
                rows = pl.ds(part_side * 256, 256)
                total = own(slot, rows)
                if part_side == side:
                    total = total + relayed[g, rows, :].astype(F32)
                outgo[slot, rows, :] = total.astype(BF16)
            r_copy(g, side).start()

    def summed(g, rows):
        total = own(4 * g + 3, rows)
        for side in range(2):
            total = total + landed[g, side, rows, :].astype(F32)
        return total

    def ry_copy():
        return remote(rsend, rland, ry_s.at[0], ry_r.at[0], m, chip_at(4) * 2 + core)

    def own(r, rows):
        return part[r, rows, lanes(core * 128, 128)] + half[r, rows, :]

    def adjoint(r, carry):
        @pl.when(r < 6)
        def _():
            load(r + 2).start()

        with scope("bwait"):
            load(r).wait()
        slot = slot_at(r)
        rows = pl.ds(pl.multiple_of(slot * 256, 256), 256)
        with scope("adot"):
            part[slot] = lax.dot_general(
                weighted[...], basis[rows, :], NT, preferred_element_type=F32
            )
        x_copy(slot).start()

        @pl.when(r > 0)
        def _():
            with scope("xwait"):
                x_copy(slot_at(r - 1)).wait_recv()

        @pl.when(r == 0)
        def _():
            with scope("p1wait"):
                to_z(inverse, zpair, zout, zland, z_s, z_r)

        @pl.when(r == 1)
        def _():
            pass_half(0)
            with scope("z0wait"):
                to_mate(inverse, zall, ysend, ypart, z_s, z_r)

        @pl.when(r == 3)
        def _():
            with scope("s0wait"):
                settle(0)
            launch_y(0)
            launch_x(0)
            with scope("c0wait"):
                combine(0)

        @pl.when(r == 4)
        def _():
            with scope("s1wait"):
                settle(1)
            launch_y(1)

        @pl.when(r == 5)
        def _():
            with scope("mate0wait"):
                relay_mate(0)
            launch_x(1)
            pass_half(1)

        @pl.when(r == 6)
        def _():
            with scope("row0wait"):
                relay_row(0)

        return carry

    lax.fori_loop(0, 8, adjoint, 0)
    with scope("mate1wait"):
        relay_mate(1)

    def i_copy(h, i, y):
        return remote(
            inc_send.at[h, i, y], inc_land.at[h, 2 * i + yl], i_s.at[0], i_r.at[h],
            ((z + 3 - i) % 4) * 2 + y, s,
        )

    def o_copy(h, u):
        return remote(
            inc_own.at[h], inc_all.at[h, m], o_s.at[0], o_r.at[h], mem_at(u), s
        )

    def field(h, low, w):
        with scope("field"):
            f = jnp.dot(
                coefs[h][:, :, low:low + 1024].reshape(256, 1024), basis[low:low + 1024, w],
                preferred_element_type=F32,
            )
            levels = pl.ds(h * 16, 16)
            product = f.reshape(16, 16, 1024) * anom[:, levels, w].astype(F32)
            return jnp.sum(product, axis=0)

    def near(h, i):
        w = lanes(i * 1024, 1024)
        inc_acc[h, :, w] = field(h, 1024, w)

    def far(h, i):
        w = lanes(((z + 3 - i) % 4) * 1024, 1024)
        value = (field(h, 0, w) + inc_acc[h, :, w]).astype(BF16)
        for y in range(2):
            inc_send[h, i, y] = value[:, y * 512:(y + 1) * 512]

        @pl.when(i < 3)
        def _():
            for y in range(2):
                i_copy(h, i, y).start()

        @pl.when(i == 3)
        def _():
            i_copy(h, i, 1 - yl).start()

    def reduce_own(h):
        total = inc_send[h, 3, yl].astype(F32)
        wait_all(inc_land.at[h, pl.ds(0, 7)], i_r.at[h])
        for k in range(6):
            total = total + inc_land[h, k].astype(F32)
        total = total + inc_land[h, 7 - yl].astype(F32)
        inc_own[h] = total.astype(BF16)
        for u in (5, 4, 3, 7, 1, 2, 6):
            o_copy(h, u).start()

    def near0(i, carry):
        near(0, i)

        @pl.when(i == 1)
        def _():
            with scope("rfwait"):
                wait_all(landed.at[0], r_r.at[0])
            for g in range(4):
                rows = pl.ds(g * 128, 128)
                rsend[rows, :] = summed(0, rows)
            ry_copy().start()

        @pl.when(i == 3)
        def _():
            with scope("rest0wait"):
                relay_rest(0)

        return carry

    def far0(i, carry):
        far(0, i)

        @pl.when(i == 1)
        def _():
            with scope("row1wait"):
                relay_row(1)
            with scope("c1wait"):
                combine(1)

        return carry

    def near1(i, carry):
        near(1, i)

        @pl.when(i == 2)
        def _():
            with scope("rest1wait"):
                relay_rest(1)

        return carry

    def far1(i, carry):
        far(1, i)

        @pl.when(i == 1)
        def _():
            with scope("i0wait"):
                reduce_own(0)

        return carry

    with scope("dn0wait"):
        gathered(0, False)
    lax.fori_loop(0, 4, near0, 0)
    with scope("df0wait"):
        gathered(0, True)
    lax.fori_loop(0, 4, far0, 0)
    with scope("dn1wait"):
        gathered(1, False)
    lax.fori_loop(0, 4, near1, 0)
    with scope("rnwait"):
        x_copy(7).wait_recv()
        wait_all(landed.at[1], r_r.at[1])
        ry_copy().wait_recv()
    for g in range(4):
        rows = pl.ds(g * 128, 128)
        total = summed(1, rows) + rland[rows, :]
        value = jnp.dot(rooted.T, total, precision=HIGH, preferred_element_type=F32) * gain
        spread(gall, gpair, g, value)
    depart(gall, gpair, gz_s, gz_r)
    with scope("df1wait"):
        gathered(1, True)
    lax.fori_loop(0, 4, far1, 0)

    with scope("gp1wait"):
        to_z(order, gpair, gout, gland, gz_s, gz_r)
    with scope("gz0wait"):
        to_mate(order, gall, gsend, gpart, gz_s, gz_r)
    with scope("i1wait"):
        reduce_own(1)
    for h in (1, 0):
        with scope("gs%dwait" % h):
            for i, value in arrived(order, h, gall, gsend, gpart, gland, gz_s, gz_r):
                ag_out[i, pl.ds(h * 16, 16), :] = value.astype(F32)

    for h in range(2):
        levels = pl.ds(h * 16, 16)
        inc_out[levels, lanes(m * 512, 512)] = inc_own[h].astype(F32)
        with scope("owait"):
            wait_all(inc_all.at[h, pl.ds(0, 7)], o_r.at[h])
        for u in range(1, 8):
            spot = mem_at(u)
            inc_out[levels, lanes(spot * 512, 512)] = inc_all[h, spot].astype(F32)

    with scope("sentwait"):
        for all_ref, src, dst, pair, send, recv in (
            (zall, ysend, ypart, zpair, z_s, z_r), (gall, gsend, gpart, gpair, gz_s, gz_r)
        ):
            wait_all(all_ref.at[pl.ds(0, 48)], send.at[0])
            y_copy(src, dst, send, recv).wait_send()
            pair_copy(pair, send, recv).wait_send()
            wait_all(all_ref.at[pl.ds(0, 48)], send.at[3])
        wait_all(coefs0.at[pl.ds(0, 14)], b_s.at[0])
        wait_all(coefs0, d_s.at[0])
        wait_all(inc_land.at[:, pl.ds(0, 7)], i_s.at[0])
        wait_all(inc_land.at[:, pl.ds(0, 7)], o_s.at[0])
        wait_all(relayed, rd_s.at[0])
        wait_all(landed, r_s.at[0])
        wait_all(half, x_s.at[0])
        ry_copy().wait_send()


def on_device(anomalies, alpha, basis, gradient, vertical_root, band_gain, band, order):
    vmem = pl.BlockSpec(memory_space=pltpu.VMEM)
    hbm = pl.BlockSpec(memory_space=pl.ANY)
    dma = lambda n: pltpu.SemaphoreType.DMA((n,))
    int32 = jnp.int32
    return pl.pallas_call(
        kernel,
        out_shape=(
            pltpu.VMEM((32, 4096), F32),
            pltpu.VMEM((16, 32, 128), F32),
        ),
        in_specs=[hbm] * 8,
        out_specs=(vmem, vmem),
        scratch_shapes=[
            pltpu.VMEM((1, 128), int32),
            pltpu.SMEM((1, 128), int32),
            pltpu.VMEM((8, 128), int32),
            pltpu.SMEM((8, 128), int32),
            pltpu.SMEM((1, 16), F32),
            pltpu.VMEM((16, 32, 128), BF16),
            pltpu.VMEM((32, 4096), BF16),
            pltpu.VMEM((32, 32), F32),
            pltpu.VMEM((1, 128), int32),
            pltpu.VMEM((2048, 4096), BF16),
            pltpu.VMEM((16, 32, 4096), BF16),
            pltpu.VMEM((512, 4096), BF16),
            pltpu.VMEM((8, 512, 256), F32),
            pltpu.VMEM((8, 512, 128), F32),
            pltpu.VMEM((7, 512, 128), BF16),
            pltpu.VMEM((2, 512, 128), BF16),
            pltpu.VMEM((2, 2, 512, 128), BF16),
            pltpu.VMEM((512, 128), F32),
            pltpu.VMEM((512, 128), F32),
            pltpu.VMEM((16, 16, 2048), BF16),
            pltpu.VMEM((16, 16, 2048), BF16),
            pltpu.VMEM((64, 16, 128), BF16),
            pltpu.VMEM((16, 16, 128), BF16),
            pltpu.VMEM((16, 16, 128), BF16),
            pltpu.VMEM((32, 16, 128), BF16),
            pltpu.VMEM((3, 16, 16, 128), BF16),
            pltpu.VMEM((64, 16, 128), BF16),
            pltpu.VMEM((2, 16, 4096), F32),
            pltpu.VMEM((2, 4, 2, 16, 512), BF16),
            pltpu.VMEM((2, 8, 16, 512), BF16),
            pltpu.VMEM((2, 16, 512), BF16),
            pltpu.VMEM((2, 8, 16, 512), BF16),
            pltpu.VMEM((64, 16, 128), BF16),
            pltpu.VMEM((16, 16, 128), BF16),
            pltpu.VMEM((16, 16, 128), BF16),
            pltpu.VMEM((32, 16, 128), BF16),
            pltpu.VMEM((3, 16, 16, 128), BF16),
            pltpu.VMEM((64, 16, 128), BF16),
            dma(8), dma(8), dma(4), dma(4), dma(4), dma(1), dma(2), dma(2), dma(2),
            dma(1), dma(4), dma(1), dma(8), dma(1), dma(2), dma(1), dma(2), dma(1), dma(1), dma(1),
            dma(2), dma(1), dma(2), dma(4), dma(4),
        ],
        compiler_params=pltpu.CompilerParams(
            collective_id=0, has_side_effects=True, vmem_limit_bytes=60 << 20
        ),
    )(
        order.reshape(1, -1), band_gain.reshape(1, -1), anomalies, alpha, basis, gradient,
        vertical_root, band.reshape(1, -1),
    )


def solution(mesh):
    return jax.shard_map(
        on_device,
        mesh=mesh,
        in_specs=(
            P("mem", None, "state"),
            P("mem", None, "state"),
            P(None, "state"),
            P(None, "state"),
            P(),
            P(),
            P("state"),
            P(),
        ),
        out_specs=(P(None, "state"), P("mem", None, "state")),
        check_vma=False,
    )
```

time: 56 us -> 50.7 us (0.905)
  Pallas kernels: 53.4 us -> 48.5 us
    pallas_call x1, Pallas kernels: 53.4 us -> 48.5 us  [on_device(): pl.pallas_call(kernel, out_shape=(pltpu.VMEM((32, 4096), F32), pltpu.VMEM...]
where the time goes in v4:
time: 50.7 us; the launch traced here: 50.6 us
  Pallas kernels  48.5 us (96%)
  local copies, waits for them, and re-layouts  1.5 us (3%)
  between operations  0.64 us (1%)
    pallas_call x1, Pallas kernels, on_device(): pl.pallas_call(kernel, out_shape=(pltpu.VMEM((32, 4096), F32), pltpu.VMEM...  48.5 us
    unnamed x2, local copies, waits for them, and re-layouts  1.5 us

profile of v4, /device:TPU:0, one launch (start us, length us, event | category | flops | bytes accessed | tf_op | source)
XLA Modules:
  0.0 50.6 jit_solution(8831173518649258292)
XLA Ops:
  0.6 48.5 %shard_map.95 = (f32[32,4096]{1,0:T(8,128)S(1)}, f32[16,32,128]{2,1,0:T(8,128)S(1)}) custom-call(s32[1,128]{1,0:T(1,128)} %bitcast.3, f32[1,16]{1,0:T(1,128)} %bitcast.4, bf16[16,32,4096]{2,1,0:T(8,128)(2,1)} %anom_hbm.1, bf16[16,32,128]{2,1,0:T(8,128)(2,1)} %alpha_hbm.1, bf16[2048,4096]{1,0:T(8,128)(2,1)} %basis_hbm.1, bf16[32,4096]{1,0:T(8,128)(2,1)} %grad_hbm.1, ...), custom_call_target="tpu_custom_call" | custom-call | tf_op jit(solution)/shard_map/pallas_call | solution.py:542
  49.1 0.8 %copy.12 = f32[32,4096]{1,0:T(8,128)} copy(f32[32,4096]{1,0:T(8,128)S(1)} %get-tuple-element.2) | data formatting | bytes 1048576
  49.9 0.7 %copy.13 = f32[16,32,128]{2,1,0:T(8,128)} copy(f32[16,32,128]{2,1,0:T(8,128)S(1)} %get-tuple-element.3) | data formatting | bytes 524288

commit v5 on v4

--- a/solution.py
+++ b/solution.py
@@ -264,6 +264,9 @@
             part.at[r, :, lanes(other * 128, 128)], half.at[r], x_s.at[0], x_r.at[r], m, partner
         )
 
+    def came(slot):
+        x_copy(slot).wait_recv()
+
     def rd_copy(g, side):
         rows = pl.ds(side * 256, 256)
         return remote(
@@ -323,21 +326,15 @@
             )
         x_copy(slot).start()
 
-        @pl.when(r > 0)
-        def _():
+        @pl.when(r == 1)
+        def _():
+            with scope("z0wait"):
+                to_mate(inverse, zall, ysend, ypart, z_s, z_r)
             with scope("xwait"):
-                x_copy(slot_at(r - 1)).wait_recv()
-
-        @pl.when(r == 0)
-        def _():
+                came(slot_at(0))
+            pass_half(0)
             with scope("p1wait"):
                 to_z(inverse, zpair, zout, zland, z_s, z_r)
-
-        @pl.when(r == 1)
-        def _():
-            pass_half(0)
-            with scope("z0wait"):
-                to_mate(inverse, zall, ysend, ypart, z_s, z_r)
 
         @pl.when(r == 3)
         def _():
@@ -346,6 +343,8 @@
             launch_y(0)
             launch_x(0)
             with scope("c0wait"):
+                came(slot_at(1))
+                came(slot_at(2))
                 combine(0)
 
         @pl.when(r == 4)
@@ -359,6 +358,8 @@
             with scope("mate0wait"):
                 relay_mate(0)
             launch_x(1)
+            with scope("xwait"):
+                came(slot_at(4))
             pass_half(1)
 
         @pl.when(r == 6)
@@ -428,6 +429,7 @@
         @pl.when(i == 1)
         def _():
             with scope("rfwait"):
+                came(slot_at(3))
                 wait_all(landed.at[0], r_r.at[0])
             for g in range(4):
                 rows = pl.ds(g * 128, 128)
@@ -449,6 +451,8 @@
             with scope("row1wait"):
                 relay_row(1)
             with scope("c1wait"):
+                came(slot_at(5))
+                came(slot_at(6))
                 combine(1)
 
         return carry
@@ -483,7 +487,7 @@
         gathered(1, False)
     lax.fori_loop(0, 4, near1, 0)
     with scope("rnwait"):
-        x_copy(7).wait_recv()
+        came(7)
         wait_all(landed.at[1], r_r.at[1])
         ry_copy().wait_recv()
     for g in range(4):

time: 50.7 us -> 49.3 us (0.972)
  Pallas kernels: 48.5 us -> 47.1 us
    pallas_call x1, Pallas kernels: 48.5 us -> 47.1 us  [on_device(): pl.pallas_call(kernel, out_shape=(pltpu.VMEM((32, 4096), F32), pltpu.VMEM...]
where the time goes in v5:
time: 49.3 us; the launch traced here: 49.2 us
  Pallas kernels  47.1 us (96%)
  local copies, waits for them, and re-layouts  1.5 us (3%)
  between operations  0.64 us (1%)
    pallas_call x1, Pallas kernels, on_device(): pl.pallas_call(kernel, out_shape=(pltpu.VMEM((32, 4096), F32), pltpu.VMEM...  47.1 us
    unnamed x2, local copies, waits for them, and re-layouts  1.5 us

profile of v5, /device:TPU:0, one launch (start us, length us, event | category | flops | bytes accessed | tf_op | source)
XLA Modules:
  0.0 49.2 jit_solution(16088463679041893077)
XLA Ops:
  0.6 47.1 %shard_map.95 = (f32[32,4096]{1,0:T(8,128)S(1)}, f32[16,32,128]{2,1,0:T(8,128)S(1)}) custom-call(s32[1,128]{1,0:T(1,128)} %bitcast.3, f32[1,16]{1,0:T(1,128)} %bitcast.4, bf16[16,32,4096]{2,1,0:T(8,128)(2,1)} %anom_hbm.1, bf16[16,32,128]{2,1,0:T(8,128)(2,1)} %alpha_hbm.1, bf16[2048,4096]{1,0:T(8,128)(2,1)} %basis_hbm.1, bf16[32,4096]{1,0:T(8,128)(2,1)} %grad_hbm.1, ...), custom_call_target="tpu_custom_call" | custom-call | tf_op jit(solution)/shard_map/pallas_call | solution.py:546
  47.7 0.8 %copy.12 = f32[32,4096]{1,0:T(8,128)} copy(f32[32,4096]{1,0:T(8,128)S(1)} %get-tuple-element.2) | data formatting | bytes 1048576
  48.5 0.7 %copy.13 = f32[16,32,128]{2,1,0:T(8,128)} copy(f32[16,32,128]{2,1,0:T(8,128)S(1)} %get-tuple-element.3) | data formatting | bytes 524288

commit v6 on v5

--- a/solution.py
+++ b/solution.py
@@ -113,39 +113,38 @@
         value = jnp.dot(rooted, rows, precision=HIGH, preferred_element_type=F32) * gain
         spread(zall, zpair, g, value)
 
+    with scope("bar"):
+        pl.semaphore_wait(barrier, 12)
+
+    def z_copy(all_ref, dz, send, recv):
+        mine = all_ref.at[pl.ds(z * 16, 16)]
+        return remote(mine, mine, send.at[0], recv.at[0], ((z + dz) % 4) * 2 + yl, s)
+
+    def y_copy(src, dst, send, recv):
+        return remote(src, dst, send.at[1], recv.at[1], ymate, s)
+
+    def pair_copy(pair, send, recv):
+        mine = pair.at[pl.ds(yl * 16, 16)]
+        return remote(mine, mine, send.at[2], recv.at[2], ymate, s)
+
+    def out_copy(out, land, dz, send, recv):
+        return remote(
+            out.at[dz - 1], land.at[pl.ds(z * 16, 16)], send.at[3], recv.at[3],
+            ((z + dz) % 4) * 2 + yl, s,
+        )
+
+    def depart(all_ref, pair, send, recv):
+        for dz in (2, 1, 3):
+            z_copy(all_ref, dz, send, recv).start()
+        pair_copy(pair, send, recv).start()
+
+    depart(zall, zpair, z_s, z_r)
+
     held = (order_v[...] == row).astype(F32).astype(BF16)
     slots = lax.broadcasted_iota(jnp.int32, (8, 128), 1).astype(F32).astype(BF16)
     inverse_v[...] = lax.dot_general(slots, held, NT, preferred_element_type=F32).astype(jnp.int32)
     to_scalars = pltpu.make_async_copy(inverse_v, inverse, small_sem.at[7])
     to_scalars.start()
-
-    with scope("bar"):
-        pl.semaphore_wait(barrier, 12)
-
-    def z_copy(all_ref, dz, send, recv):
-        mine = all_ref.at[pl.ds(z * 16, 16)]
-        return remote(mine, mine, send.at[0], recv.at[0], ((z + dz) % 4) * 2 + yl, s)
-
-    def y_copy(src, dst, send, recv):
-        return remote(src, dst, send.at[1], recv.at[1], ymate, s)
-
-    def pair_copy(pair, send, recv):
-        mine = pair.at[pl.ds(yl * 16, 16)]
-        return remote(mine, mine, send.at[2], recv.at[2], ymate, s)
-
-    def out_copy(out, land, dz, send, recv):
-        return remote(
-            out.at[dz - 1], land.at[pl.ds(z * 16, 16)], send.at[3], recv.at[3],
-            ((z + dz) % 4) * 2 + yl, s,
-        )
-
-    def depart(all_ref, pair, send, recv):
-        for dz in (2, 1, 3):
-            z_copy(all_ref, dz, send, recv).start()
-        pair_copy(pair, send, recv).start()
-
-    depart(zall, zpair, z_s, z_r)
-    to_scalars.wait()
 
     small(6).wait()
     for g in range(4):
@@ -156,13 +155,14 @@
 
         def weigh(c, carry):
             w = lanes(c * 512, 512)
-            factor = grad[:, w].astype(F32)
+            factor = grad[:, w]
             for k in range(4):
-                value = (anom[g * 4 + k, :, w].astype(F32) * factor).astype(BF16)
-                weighted[pl.ds(g * 128 + k * 32, 32), w] = value
+                weighted[pl.ds(g * 128 + k * 32, 32), w] = anom[g * 4 + k, :, w] * factor
             return carry
 
         lax.fori_loop(0, 8, weigh, 0)
+
+    to_scalars.wait()
 
     def held_at(table, slot):
         return jnp.bitwise_and(table[0, slot], 127)
@@ -274,10 +274,10 @@
             chip_at(1 + 2 * side) * 2 + core,
         )
 
-    def r_copy(g, side):
+    def r_copy(g, side, rows):
         slot = 4 * g + 2 - 2 * side
         return remote(
-            outgo.at[slot], landed.at[g, side], r_s.at[0], r_r.at[g], m,
+            outgo.at[slot, rows], landed.at[g, side, rows], r_s.at[0], r_r.at[g], m,
             chip_at(1 + 2 * side) * 2 + core,
         )
 
@@ -287,17 +287,20 @@
         for side in range(2):
             rd_copy(g, side).start()
 
+    def alone(g, side):
+        slot = 4 * g + 2 - 2 * side
+        rows = pl.ds((1 - side) * 256, 256)
+        outgo[slot, rows, :] = own(slot, rows).astype(BF16)
+        r_copy(g, side, rows).start()
+
     def combine(g):
         wait_all(relayed.at[g], rd_r.at[g])
         for side in range(2):
             slot = 4 * g + 2 - 2 * side
-            for part_side in range(2):
-                rows = pl.ds(part_side * 256, 256)
-                total = own(slot, rows)
-                if part_side == side:
-                    total = total + relayed[g, rows, :].astype(F32)
-                outgo[slot, rows, :] = total.astype(BF16)
-            r_copy(g, side).start()
+            rows = pl.ds(side * 256, 256)
+            total = own(slot, rows) + relayed[g, rows, :].astype(F32)
+            outgo[slot, rows, :] = total.astype(BF16)
+            r_copy(g, side, rows).start()
 
     def summed(g, rows):
         total = own(4 * g + 3, rows)
@@ -336,15 +339,20 @@
             with scope("p1wait"):
                 to_z(inverse, zpair, zout, zland, z_s, z_r)
 
+        @pl.when(r == 2)
+        def _():
+            came(slot_at(1))
+            alone(0, 0)
+
         @pl.when(r == 3)
         def _():
+            came(slot_at(2))
+            alone(0, 1)
             with scope("s0wait"):
                 settle(0)
             launch_y(0)
             launch_x(0)
             with scope("c0wait"):
-                came(slot_at(1))
-                came(slot_at(2))
                 combine(0)
 
         @pl.when(r == 4)
@@ -372,6 +380,9 @@
     lax.fori_loop(0, 8, adjoint, 0)
     with scope("mate1wait"):
         relay_mate(1)
+    for side in range(2):
+        came(slot_at(5 + side))
+        alone(1, side)
 
     def i_copy(h, i, y):
         return remote(
@@ -451,8 +462,6 @@
             with scope("row1wait"):
                 relay_row(1)
             with scope("c1wait"):
-                came(slot_at(5))
-                came(slot_at(6))
                 combine(1)
 
         return carry
@@ -464,6 +473,19 @@
         def _():
             with scope("rest1wait"):
                 relay_rest(1)
+
+        @pl.when(i == 2)
+        def _():
+            with scope("rnwait"):
+                came(7)
+                wait_all(landed.at[1], r_r.at[1])
+                ry_copy().wait_recv()
+            for g in range(4):
+                rows = pl.ds(g * 128, 128)
+                total = summed(1, rows) + rland[rows, :]
+                value = jnp.dot(rooted.T, total, precision=HIGH, preferred_element_type=F32) * gain
+                spread(gall, gpair, g, value)
+            depart(gall, gpair, gz_s, gz_r)
 
         return carry
 
@@ -486,16 +508,6 @@
     with scope("dn1wait"):
         gathered(1, False)
     lax.fori_loop(0, 4, near1, 0)
-    with scope("rnwait"):
-        came(7)
-        wait_all(landed.at[1], r_r.at[1])
-        ry_copy().wait_recv()
-    for g in range(4):
-        rows = pl.ds(g * 128, 128)
-        total = summed(1, rows) + rland[rows, :]
-        value = jnp.dot(rooted.T, total, precision=HIGH, preferred_element_type=F32) * gain
-        spread(gall, gpair, g, value)
-    depart(gall, gpair, gz_s, gz_r)
     with scope("df1wait"):
         gathered(1, True)
     lax.fori_loop(0, 4, far1, 0)
@@ -538,12 +550,23 @@
         ry_copy().wait_send()
 
 
+def write_out(inc, ag, inc_out, ag_out, sem):
+    copies = [
+        pltpu.make_async_copy(inc, inc_out, sem.at[0]),
+        pltpu.make_async_copy(ag, ag_out, sem.at[1]),
+    ]
+    for copy in copies:
+        copy.start()
+    for copy in copies:
+        copy.wait()
+
+
 def on_device(anomalies, alpha, basis, gradient, vertical_root, band_gain, band, order):
     vmem = pl.BlockSpec(memory_space=pltpu.VMEM)
     hbm = pl.BlockSpec(memory_space=pl.ANY)
     dma = lambda n: pltpu.SemaphoreType.DMA((n,))
     int32 = jnp.int32
-    return pl.pallas_call(
+    inc, ag = pl.pallas_call(
         kernel,
         out_shape=(
             pltpu.VMEM((32, 4096), F32),
@@ -601,6 +624,18 @@
         order.reshape(1, -1), band_gain.reshape(1, -1), anomalies, alpha, basis, gradient,
         vertical_root, band.reshape(1, -1),
     )
+    inc = pltpu.with_memory_space_constraint(inc, pltpu.VMEM)
+    ag = pltpu.with_memory_space_constraint(ag, pltpu.VMEM)
+    return pl.pallas_call(
+        write_out,
+        out_shape=(
+            jax.ShapeDtypeStruct((32, 4096), F32),
+            jax.ShapeDtypeStruct((16, 32, 128), F32),
+        ),
+        in_specs=[vmem] * 2,
+        out_specs=(hbm, hbm),
+        scratch_shapes=[dma(2)],
+    )(inc, ag)
 
 
 def solution(mesh):

time: 49.3 us -> 48.7 us (0.988)
  local copies, waits for them, and re-layouts: 1.5 us -> 0 us
  Pallas kernels: 47.1 us -> 48 us
    unnamed x2 -> x0, local copies, waits for them, and re-layouts: 1.5 us -> none
    pallas_call x0 -> x1, Pallas kernels: none -> 0.89 us  [on_device(): pl.pallas_call(write_out, out_shape=(jax.ShapeDtypeStruct((32, 4096), F32...]
where the time goes in v6:
time: 48.7 us; the launch traced here: 48.6 us
  Pallas kernels  48 us (99%)
  between operations  0.64 us (1%)
    pallas_call x1, Pallas kernels, on_device(): pl.pallas_call(kernel, out_shape=(pltpu.VMEM((32, 4096), F32), pltpu.VMEM...  47.1 us

profile of v6, /device:TPU:0, one launch (start us, length us, event | category | flops | bytes accessed | tf_op | source)
XLA Modules:
  0.0 48.6 jit_solution(7159717579891398109)
XLA Ops:
  0.6 47.1 %shard_map.95 = (f32[32,4096]{1,0:T(8,128)S(1)}, f32[16,32,128]{2,1,0:T(8,128)S(1)}) custom-call(s32[1,128]{1,0:T(1,128)} %bitcast.3, f32[1,16]{1,0:T(1,128)} %bitcast.4, bf16[16,32,4096]{2,1,0:T(8,128)(2,1)} %anom_hbm.1, bf16[16,32,128]{2,1,0:T(8,128)(2,1)} %alpha_hbm.1, bf16[2048,4096]{1,0:T(8,128)(2,1)} %basis_hbm.1, bf16[32,4096]{1,0:T(8,128)(2,1)} %grad_hbm.1, ...), custom_call_target="tpu_custom_call" | custom-call | tf_op jit(solution)/shard_map/pallas_call | solution.py:569
  47.7 0.9 %shard_map.96 = (f32[32,4096]{1,0:T(8,128)}, f32[16,32,128]{2,1,0:T(8,128)}) custom-call(f32[32,4096]{1,0:T(8,128)S(1)} %get-tuple-element.4.inc, f32[16,32,128]{2,1,0:T(8,128)S(1)} %get-tuple-element.5.ag), custom_call_target="tpu_custom_call" | custom-call | tf_op jit(solution)/shard_map/pallas_call | solution.py:629

commit v7 on v6

--- a/solution.py
+++ b/solution.py
@@ -447,7 +447,7 @@
                 rsend[rows, :] = summed(0, rows)
             ry_copy().start()
 
-        @pl.when(i == 3)
+        @pl.when(i == 2)
         def _():
             with scope("rest0wait"):
                 relay_rest(0)

time: 48.7 us -> 48.7 us (level)
  no operation moved by 1% of the time
where the time goes in v7:
time: 48.7 us; the launch traced here: 48.6 us
  Pallas kernels  47.9 us (98%)
  between operations  0.64 us (1%)
    pallas_call x1, Pallas kernels, on_device(): pl.pallas_call(kernel, out_shape=(pltpu.VMEM((32, 4096), F32), pltpu.VMEM...  47 us

profile of v7, /device:TPU:0, one launch (start us, length us, event | category | flops | bytes accessed | tf_op | source)
XLA Modules:
  0.0 48.6 jit_solution(6774073154970878892)
XLA Ops:
  0.6 47.0 %shard_map.95 = (f32[32,4096]{1,0:T(8,128)S(1)}, f32[16,32,128]{2,1,0:T(8,128)S(1)}) custom-call(s32[1,128]{1,0:T(1,128)} %bitcast.3, f32[1,16]{1,0:T(1,128)} %bitcast.4, bf16[16,32,4096]{2,1,0:T(8,128)(2,1)} %anom_hbm.1, bf16[16,32,128]{2,1,0:T(8,128)(2,1)} %alpha_hbm.1, bf16[2048,4096]{1,0:T(8,128)(2,1)} %basis_hbm.1, bf16[32,4096]{1,0:T(8,128)(2,1)} %grad_hbm.1, ...), custom_call_target="tpu_custom_call" | custom-call | tf_op jit(solution)/shard_map/pallas_call | solution.py:569
  47.7 0.9 %shard_map.96 = (f32[32,4096]{1,0:T(8,128)}, f32[16,32,128]{2,1,0:T(8,128)}) custom-call(f32[32,4096]{1,0:T(8,128)S(1)} %get-tuple-element.4.inc, f32[16,32,128]{2,1,0:T(8,128)S(1)} %get-tuple-element.5.ag), custom_call_target="tpu_custom_call" | custom-call | tf_op jit(solution)/shard_map/pallas_call | solution.py:629
